TPU v7x, 256 devices: a whole 4x4x8 slice. The times are simulated.
256 devices in a mesh: dp: 64 (over z_lo, x, y, core), vocab: 4 (over z_hi).
Axes of the slice: x: 4, y: 4, z: 8 (z_hi: 4, z_lo: 2; z = z_hi * 2 + z_lo), core: 2. Of those that a mesh axis runs over, the one named last changes fastest.
Arguments:
- hidden: bfloat16 [512, 4096], P('dp'), may hold values from -16 to 16
- embed_grad: bfloat16 [512, 4096], P('dp'), may hold values from -8 to 8
- token_ids: int32 [512], P('dp'), may hold values from 0 to 32767
- loss_weight: float32 [512], P('dp'), may hold values from 16 to 256
- teacher_logits: bfloat16 [512, 32768], P('dp', 'vocab'), may hold values from -24 to 256
- head: bfloat16 [4096, 32768], P('dp', 'vocab'), may hold values from -1 to 1
Outputs:
- grad_hidden: bfloat16 [512, 4096], P('dp', 'vocab')
- head_grad: float32 [4096, 32768], P('dp', 'vocab')
Inputs may be any that keep to these rules, and one draw needn't show every extreme that they name: `token_ids`: token ids of the vocabulary window.
All inputs are finite; a program needn't handle non-finite values.
Results may differ from a plain program's by a relative error of at most 0.0022.
The roundings to bfloat16 on the way count: a program that leaves them out, or rounds other values in their place, can miss the bound.
Values may be sent and summed in bfloat16 or wider, within the bound.
No kernel may reach another device: no remote copies, remote signals or barrier semaphores. Data moves between devices by JAX's collectives and lax.ppermute only.
A program may use at most 128 MiB of HBM per device.

v0:
```python
import functools

import jax
import jax.numpy as jnp
from jax import lax
from jax.experimental import pallas as pl
from jax.experimental.pallas import tpu as pltpu
from jax.sharding import Mesh
from jax.sharding import PartitionSpec as P


DP = ("z", "x", "y", "c")
COLS = ("z", "x", "c")
FIT = 64.0
SMEM = pl.BlockSpec(memory_space=pltpu.SMEM)
VMEM = pl.BlockSpec(memory_space=pltpu.VMEM)
HBM = pl.BlockSpec(memory_space=pltpu.MemorySpace.HBM)


def exchange(x, axes):
    return lax.all_to_all(x, axes, 0, 0, tiled=True)


def shifted(x, axis, step):
    size = lax.axis_size(axis)
    return lax.ppermute(x, axis, [(k, (k + step) % size) for k in range(size)])


def shifted_both(x, z_step, x_step):
    nz, nx = lax.axis_size("z"), lax.axis_size("x")
    pairs = [
        (z * nx + k, (z + z_step) % nz * nx + (k + x_step) % nx)
        for z in range(nz)
        for k in range(nx)
    ]
    return lax.ppermute(x, ("z", "x"), pairs)


def dot(left, right, contract):
    return lax.dot_general(left, right, (contract, ((), ())), preferred_element_type=jnp.float32)


def call(body, outs, scratch=(), ins=None):
    def run(place, *operands):
        specs = list(ins or [VMEM] * len(operands))
        operands = [
            pltpu.with_memory_space_constraint(x, pltpu.MemorySpace.HBM) if spec is not VMEM else x
            for x, spec in zip(operands, specs)
        ]
        return pl.pallas_call(
            body,
            out_shape=[spec.memory_space(out.shape, out.dtype) for out, spec in outs],
            in_specs=[SMEM] + specs,
            out_specs=[spec for _, spec in outs],
            scratch_shapes=list(scratch),
            compiler_params=pltpu.CompilerParams(vmem_limit_bytes=16 << 20),
        )(place, *operands)

    return run


def held(shape, dtype):
    return jax.ShapeDtypeStruct(shape, dtype), VMEM


def stored(shape, dtype):
    return jax.ShapeDtypeStruct(shape, dtype), HBM


def joined(x):
    top = jnp.max(x, axis=0)
    return top + jnp.log(jnp.sum(jnp.exp(x - top), axis=0))


def position(place, sizes):
    _, nx, ny, nc, nv = sizes
    at = place[0] // nv
    c = lax.rem(at, nc)
    y = lax.rem(at // nc, ny)
    x = lax.rem(at // (nc * ny), nx)
    return at // (nc * ny * nx), x, y, c


def row_of(where, sizes, dc, dx, dz):
    nz, nx, _, nc, _ = sizes
    z = lax.rem(where[0] + (nz - dz), nz)
    x = lax.rem(where[1] + (nx - dx), nx)
    c = lax.rem(where[3] + (nc - dc), nc)
    return (z * nx + x) * nc + c


def send_kernel(place, ids, weights, hidden, embed, head, teacher, *refs, sizes):
    nz, nx, ny, _, _ = sizes
    stacked, outs = refs[0], refs[1 : 1 + ny]
    hidden_here, embed_here, sems = refs[1 + ny :]
    _, _, y, _ = position(place, sizes)
    rows, own = head.shape[0], teacher.shape[0]
    cols, _, block = stacked.shape
    step = hidden.shape[1] // (nz * nx * ny)
    moves = [(hidden, hidden_here), (embed, embed_here)]
    for j in range(cols):
        lanes = slice(j * block, (j + 1) * block)
        moves.append((head.at[:, lanes], stacked.at[j, :rows, :]))
        moves.append((teacher.at[:, lanes], stacked.at[j, rows : rows + own, :]))
    moves = [pltpu.make_async_copy(*move, sems.at[k]) for k, move in enumerate(moves)]
    for move in moves:
        move.start()
    line = lax.broadcasted_iota(jnp.int32, (own, 128), 0)
    lane = lax.broadcasted_iota(jnp.int32, (own, 128), 1)
    weight = jnp.zeros((own, 128), jnp.float32)
    number = jnp.zeros((own, 128), jnp.int32)
    for t in range(own):
        weight = jnp.where(line == t, weights[t], weight)
        number = jnp.where(line == t, ids[t], number)
    number = jnp.where(lane == rows, number // 256, lax.rem(number, 256))
    number = jnp.where((lane == rows) | (lane == rows + 1), number, 0)
    number = number.astype(jnp.float32).astype(jnp.bfloat16)
    for q in range(block // 128):
        piece = weight.astype(jnp.bfloat16)
        weight = weight - piece.astype(jnp.float32)
        for j in range(cols):
            stacked[j, rows + own :, q * 128 : (q + 1) * 128] = piece
    moves[0].wait()
    moves[1].wait()
    for k, out in enumerate(outs):
        to = lax.rem(y + k, ny)
        for g in range(nz * nx):
            lanes = pl.ds(pl.multiple_of((g * ny + to) * step, step), step)
            out[:, g * step : (g + 1) * step] = hidden_here[:, lanes]
            out[:, (nz * nx + g) * step : (nz * nx + g + 1) * step] = embed_here[:, lanes]
        out[:, 2 * nz * nx * step :] = number
    for move in moves[2:]:
        move.wait()


def student_kernel(place, same, other, stacked, *refs, sizes, own, rows):
    where = position(place, sizes)
    nz, nx, ny, nc, _ = sizes
    outs, kept, head, sem = refs[:ny], refs[ny], refs[ny + 1], refs[ny + 2]
    for j in range(nz * nx * nc):
        head[j * rows : (j + 1) * rows, :] = stacked[j, :rows, :]
    keep = pltpu.make_async_copy(head, kept, sem)
    keep.start()
    for dc, half in enumerate((same, other)):
        made = jnp.dot(half[...], head[...], preferred_element_type=jnp.float32)
        at = 0
        for dx in range(nx):
            for dz in range(nz):
                row = pl.multiple_of(row_of(where, sizes, dc, dx, dz) * own, own)
                for k in range(ny):
                    outs[k][pl.ds(row, own), :] = made[at : at + own, :]
                    at += own
    keep.wait()


def back_kernel(place, g0, g1, g2, g3, kept, same, other, gap, head, sem, *, sizes, own):
    where = position(place, sizes)
    nz, nx, _, nc, _ = sizes
    fetch = pltpu.make_async_copy(kept, head, sem)
    fetch.start()
    at = 0
    for dc in range(nc):
        for dx in range(nx):
            for dz in range(nz):
                row = pl.multiple_of(row_of(where, sizes, dc, dx, dz) * own, own)
                for part in (g0, g1, g2, g3):
                    gap[at : at + own, :] = part[pl.ds(row, own), :]
                    at += own
    half = at // nc
    fetch.wait()
    for dc, out in ((1, other), (0, same)):
        out[...] = lax.dot_general(
            gap[dc * half : (dc + 1) * half, :],
            head[...],
            (((1,), (1,)), ((), ())),
            preferred_element_type=jnp.float32,
        )


def arrange_kernel(place, *refs, sizes):
    _, _, ny, _, nv = sizes
    _, _, y, _ = position(place, sizes)
    v = lax.rem(place[0], nv)
    parts, outs = refs[:ny], refs[ny:]
    width = parts[0].shape[1] // nv
    for k, out in enumerate(outs):
        start = lax.rem(v + k, nv) * width
        for j, part in enumerate(parts):
            for g in range(width // 128):
                to = pl.multiple_of((g * ny + lax.rem(y + j, ny)) * 128, 128)
                out[:, pl.ds(to, 128)] = part[
                    :, pl.ds(pl.multiple_of(start + g * 128, 128), 128)
                ]


def head_kernel(place, dense, along, result, mine, out, sems, *, sizes):
    rows, block = out.shape[0], dense.shape[2]
    own = along.shape[1]
    at = 0
    for y in range(block // 128):
        for j in range(dense.shape[0]):
            mine[at : at + own, :] = along[j, :, y * 128 : (y + 1) * 128]
            at += own
    numbers = mine[:, rows : rows + 2].astype(jnp.float32)
    ids = (numbers[:, :1] * 256 + numbers[:, 1:]).astype(jnp.int32)
    ids = ids - lax.rem(place[0], sizes[4]) * out.shape[1]
    spots = lax.broadcasted_iota(jnp.int32, (at, block), 1)
    moves = []
    for j in range(dense.shape[0]):
        found = jnp.where(ids - j * block == spots, 1.0, 0.0).astype(jnp.bfloat16)
        made = lax.dot_general(
            mine[:, :rows], found, (((0,), (0,)), ((), ())), preferred_element_type=jnp.float32
        )
        lanes = slice(j * block, (j + 1) * block)
        out[:, lanes] = made + dense[j].astype(jnp.float32)
        moves.append(pltpu.make_async_copy(out.at[:, lanes], result.at[:, lanes], sems.at[j]))
        moves[j].start()
    for move in moves:
        move.wait()


def per_device(hidden, embed_grad, token_ids, loss_weight, teacher_logits, head):
    bf16, f32, f16 = jnp.bfloat16, jnp.float32, jnp.float16
    shape = tuple(lax.axis_size(axis) for axis in DP + ("vocab",))
    nz, nx, ny, nc, nv = shape
    own, width = hidden.shape
    rows, vocab = head.shape
    cols = nz * nx * nc
    block = vocab // cols
    tokens = cols * ny * own
    part = cols * rows
    group = cols * own
    place = lax.axis_index(DP + ("vocab",)).astype(jnp.int32).reshape(1)

    stacked, *pieces = call(
        functools.partial(send_kernel, sizes=shape),
        [held((cols, rows + 2 * own, block), bf16)] + [held((own, 2 * part + 128), bf16)] * ny,
        [pltpu.VMEM((own, width), bf16)] * 2 + [pltpu.SemaphoreType.DMA((2 + 2 * cols,))],
        [SMEM, SMEM, HBM, HBM, HBM, HBM],
    )(place, token_ids, loss_weight, hidden, embed_grad, head, teacher_logits)
    stacked = exchange(stacked, COLS)
    teacher = stacked[:, rows : rows + own].reshape(group, block).astype(f32)
    weights = stacked[:, rows + own :, :: block // 4].reshape(group, 4).astype(f32)
    weights = weights[:, 0] + weights[:, 1] + weights[:, 2] + weights[:, 3]

    line = [pieces[0]] + [shifted(pieces[k], "y", k) for k in range(1, ny)]
    embed_part = jnp.stack([piece[:, part:] for piece in line])
    line = jnp.concatenate([piece[:, :part] for piece in line], axis=0)
    steps = [(dz, dx) for dx in range(nx) for dz in range(nz)][1:]
    same = jnp.concatenate([line] + [shifted_both(line, *step) for step in steps], axis=0)
    other = shifted(same, "c", 1)

    *partials, head_part = call(
        functools.partial(student_kernel, sizes=shape, own=own, rows=rows),
        [held((group, block), f32)] * ny + [stored((part, block), bf16)],
        [pltpu.VMEM((part, block), bf16), pltpu.SemaphoreType.DMA],
    )(place, same, other, stacked)
    student = partials[0]
    for k in range(1, ny):
        student = student + shifted(partials[k], "y", -k)

    along = jnp.concatenate(
        [
            embed_part[:, :, :part].reshape(ny, own, cols, rows),
            jnp.broadcast_to(embed_part[:, :, None, part + rows :], (ny, own, cols, 128 - rows)),
        ],
        axis=3,
    )
    along = along.transpose(2, 1, 0, 3).reshape(cols, own, ny * 128)
    along = exchange(along, COLS)

    student_max = jnp.max(student, axis=1)
    teacher_max = jnp.max(teacher, axis=1)
    student_sum = jnp.sum(jnp.exp(student - student_max[:, None]), axis=1)
    teacher_sum = jnp.sum(jnp.exp(teacher - teacher_max[:, None]), axis=1)
    stats = jnp.stack(
        [student_max + jnp.log(student_sum), teacher_max + jnp.log(teacher_sum)]
    )
    stats = jnp.broadcast_to(stats[None], (cols * nv, *stats.shape))
    stats, along = lax.optimization_barrier((stats, along))
    norms = joined(exchange(stats, COLS + ("vocab",)))
    gap = (
        weights[:, None]
        * (jnp.exp(student - norms[0][:, None]) - jnp.exp(teacher - norms[1][:, None]))
    ).astype(bf16)
    gaps = [gap] + [shifted(gap, "y", k) for k in range(1, ny)]

    half = tokens // nc
    back, back_other, gap_all = call(
        functools.partial(back_kernel, sizes=shape, own=own),
        [held((half, part), f32), held((half, part), f32), held((tokens, block), bf16)],
        [pltpu.VMEM((part, block), bf16), pltpu.SemaphoreType.DMA],
        [VMEM] * ny + [HBM],
    )(place, *gaps, head_part)

    dense = dot(same, gap_all[:half], ((0,), (0,))) + dot(other, gap_all[half:], ((0,), (0,)))
    dense = dense.astype(bf16).reshape(cols, rows, block)

    back = back + shifted(back_other, "c", 1)
    back = back.reshape(nx * nz, ny * own, part)
    sent = (back * FIT).astype(f16)
    came = []
    for k, (dz, dx) in enumerate(steps, 1):
        came.append(shifted_both(sent[k], dz, -dx).astype(f32) * (1 / FIT))
    dense = exchange(dense, COLS)
    total = functools.reduce(jnp.add, came, back[0])
    total = total.reshape(ny, own, part)
    spread = call(
        functools.partial(arrange_kernel, sizes=shape), [held((own, width // nv), f32)] * nv
    )(place, total[0], *[shifted(total[k], "y", -k) for k in range(1, ny)])
    spread = [spread[0]] + [shifted(spread[k], "vocab", k) for k in range(1, nv)]
    head_grad = call(
        functools.partial(head_kernel, sizes=shape),
        [stored((rows, vocab), f32)],
        [pltpu.VMEM((tokens, 128), bf16), pltpu.VMEM((rows, vocab), f32), pltpu.SemaphoreType.DMA((cols,))],
    )(place, dense, along)[0]
    spread, head_grad = lax.optimization_barrier((spread, head_grad))
    grad_hidden = functools.reduce(jnp.add, spread).astype(bf16)
    return grad_hidden, head_grad


def solution(mesh):
    torus = Mesh(
        mesh.devices.reshape(2, 4, 4, 2, mesh.shape["vocab"]), ("z", "x", "y", "c", "vocab")
    )
    in_specs = (P(DP, None), P(DP, None), P(DP), P(DP), P(DP, "vocab"), P(DP, "vocab"))
    out_specs = (P(DP, "vocab"), P(DP, "vocab"))

    return jax.shard_map(
        per_device, mesh=torus, in_specs=in_specs, out_specs=out_specs, check_vma=False
    )
```

profile of v0, /device:TPU:2, one launch (start us, length us, event | category | flops | bytes accessed | tf_op | source)
XLA Modules:
  0.0 150.8 jit_solution(3488907670032463188)
XLA Ops:
  0.6 3.4 %shard_map.77 = (bf16[16,80,512]{2,1,0:T(8,128)(2,1)}, bf16[8,2176]{1,0:T(8,128)(2,1)S(1)}, bf16[8,2176]{1,0:T(8,128)(2,1)S(1)}, bf16[8,2176]{1,0:T(8,128)(2,1)S(1)}, bf16[8,2176]{1,0:T(8,128)(2,1)S(1)}) custom-call(s32[1]{0:T(128)} %bitcast.place, s32[8]{0:T(128)} %ids.1, f32[8]{0:T(128)} %weights.1, bf16[8,4096]{1,0:T(8,128)(2,1)} %hidden.1, ...), custom_call_target="tpu_custom_call" | custom-call | tf_op jit(solution)/shard_map/pallas_call | solution.py:50
  4.1 6.2 %all-to-all-start = ((bf16[16,80,512]{2,1,0:T(8,128)(2,1)}), bf16[16,80,512]{2,1,0:T(8,128)(2,1)S(1)}, u32[]{:S(2)}, u32[]{:S(2)}) async-start(bf16[16,80,512]{2,1,0:T(8,128)(2,1)} %get-tuple-element.26), calls=%async_computation | async-start | bytes 2621440 | tf_op jit(solution)/shard_map/all_to_all | solution.py:21
  11.9 2.9 %collective-permute-start.1 = (bf16[8,2176]{1,0:T(8,128)(2,1)S(1)}, bf16[8,2176]{1,0:T(8,128)(2,1)S(1)}, u32[]{:S(2)}, u32[]{:S(2)}) collective-permute-start(bf16[8,2176]{1,0:T(8,128)(2,1)S(1)} %get-tuple-element.29), channel_id=1, source_target_pairs={{0,16},{8,24},{16,0},{24,8},{1,17},{9,25},{17,1},{25,9},{2,18},{10... | collective-permute-start | bytes 104456 | tf_op jit(solution)/shard_map/ppermute | solution.py:26
  20.3 2.7 %collective-permute-start.8 = (bf16[32,1024]{1,0:T(8,128)(2,1)S(1)}, bf16[32,1024]{1,0:T(8,128)(2,1)S(1)}, u32[]{:S(2)}, u32[]{:S(2)}) collective-permute-start(bf16[32,1024]{1,0:T(8,128)(2,1)S(1)} %pad_maximum_fusion.1), channel_id=1, source_target_pairs={{0,96},{32,0},{64,32},{96,64},{128,224},{160,128},{192,160},{224,1... | collective-permute-start | bytes 196616 | tf_op jit(solution)/shard_map/ppermute | solution.py:36
  23.2 3.3 %collective-permute-start.6 = (bf16[32,1024]{1,0:T(8,128)(2,1)S(1)}, bf16[32,1024]{1,0:T(8,128)(2,1)S(1)}, u32[]{:S(2)}, u32[]{:S(2)}) collective-permute-start(bf16[32,1024]{1,0:T(8,128)(2,1)S(1)} %pad_maximum_fusion.1), channel_id=1, source_target_pairs={{0,64},{32,96},{64,0},{96,32},{128,192},{160,224},{192,128},{224,1... | collective-permute-start | bytes 196616 | tf_op jit(solution)/shard_map/ppermute | solution.py:36
  28.2 4.0 %collective-permute-done.3 = bf16[32,1024]{1,0:T(8,128)(2,1)S(1)} collective-permute-done((bf16[32,1024]{1,0:T(8,128)(2,1)S(1)}, bf16[32,1024]{1,0:T(8,128)(2,1)S(1)}, u32[]{:S(2)}, u32[]{:S(2)}) %collective-permute-start.3) | collective-permute-done | bytes 65568 | tf_op jit(solution)/shard_map/ppermute | solution.py:36
  32.8 3.7 %collective-permute-done.4 = bf16[32,1024]{1,0:T(8,128)(2,1)S(1)} collective-permute-done((bf16[32,1024]{1,0:T(8,128)(2,1)S(1)}, bf16[32,1024]{1,0:T(8,128)(2,1)S(1)}, u32[]{:S(2)}, u32[]{:S(2)}) %collective-permute-start.4) | collective-permute-done | bytes 65568 | tf_op jit(solution)/shard_map/ppermute | solution.py:36
  37.0 4.6 %collective-permute-done.5 = bf16[32,1024]{1,0:T(8,128)(2,1)S(1)} collective-permute-done((bf16[32,1024]{1,0:T(8,128)(2,1)S(1)}, bf16[32,1024]{1,0:T(8,128)(2,1)S(1)}, u32[]{:S(2)}, u32[]{:S(2)}) %collective-permute-start.5) | collective-permute-done | bytes 65568 | tf_op jit(solution)/shard_map/ppermute | solution.py:36
  42.7 5.8 %all-to-all-start.1 = ((bf16[16,8,512]{2,1,0:T(8,128)(2,1)}), bf16[16,8,512]{2,1,0:T(8,128)(2,1)S(1)}, u32[]{:S(2)}, u32[]{:S(2)}) async-start(bf16[16,8,512]{2,1,0:T(8,128)(2,1)} %maximum_bitcast_fusion), calls=%async_computation.1 | async-start | bytes 262144 | tf_op jit(solution)/shard_map/all_to_all | solution.py:21
  50.8 3.1 %collective-permute-start.11 = (f32[128,512]{1,0:T(8,128)S(1)}, f32[128,512]{1,0:T(8,128)}, u32[]{:S(2)}, u32[]{:S(2)}) collective-permute-start(f32[128,512]{1,0:T(8,128)S(1)} %get-tuple-element.32), channel_id=1, source_target_pairs={{0,24},{8,0},{16,8},{24,16},{1,25},{9,1},{17,9},{25,17},{2,26},{10... | collective-permute-start | bytes 786440 | tf_op jit(solution)/shard_map/ppermute | solution.py:26
  61.6 3.8 %collective-permute-done.11 = f32[128,512]{1,0:T(8,128)} collective-permute-done((f32[128,512]{1,0:T(8,128)S(1)}, f32[128,512]{1,0:T(8,128)}, u32[]{:S(2)}, u32[]{:S(2)}) %collective-permute-start.11) | collective-permute-done | bytes 262176 | tf_op jit(solution)/shard_map/ppermute | solution.py:26
  65.4 3.7 %collective-permute-done.13 = f32[128,512]{1,0:T(8,128)} collective-permute-done((f32[128,512]{1,0:T(8,128)S(1)}, f32[128,512]{1,0:T(8,128)}, u32[]{:S(2)}, u32[]{:S(2)}) %collective-permute-start.13) | collective-permute-done | bytes 262176 | tf_op jit(solution)/shard_map/ppermute | solution.py:26
  71.8 11.3 %all-to-all-start.2 = ((f32[64,2,128]{2,1,0:T(2,128)}), f32[64,2,128]{2,1,0:T(2,128)S(1)}, u32[]{:S(2)}, u32[]{:S(2)}) async-start(f32[64,2,128]{2,1,0:T(2,128)} %broadcast_in_dim.4), calls=%async_computation.2 | async-start | bytes 131072 | tf_op jit(solution)/shard_map/all_to_all | solution.py:21
  83.2 8.4 %all-to-all-done.2 = f32[64,2,128]{2,1,0:T(2,128)S(1)} async-done(((f32[64,2,128]{2,1,0:T(2,128)}), f32[64,2,128]{2,1,0:T(2,128)S(1)}, u32[]{:S(2)}, u32[]{:S(2)}) %all-to-all-start.2) | async-done | bytes 65568 | tf_op jit(solution)/shard_map/all_to_all | solution.py:21
  94.0 4.3 %collective-permute-done.16.g3 = bf16[128,512]{1,0:T(8,128)(2,1)S(1)} collective-permute-done((bf16[128,512]{1,0:T(8,128)(2,1)S(1)}, bf16[128,512]{1,0:T(8,128)(2,1)S(1)}, u32[]{:S(2)}, u32[]{:S(2)}) %collective-permute-start.16) | collective-permute-done | bytes 131104 | tf_op jit(solution)/shard_map/ppermute | solution.py:26
  98.3 2.2 %collective-permute-done.15.g2 = bf16[128,512]{1,0:T(8,128)(2,1)S(1)} collective-permute-done((bf16[128,512]{1,0:T(8,128)(2,1)S(1)}, bf16[128,512]{1,0:T(8,128)(2,1)S(1)}, u32[]{:S(2)}, u32[]{:S(2)}) %collective-permute-start.15) | collective-permute-done | bytes 131104 | tf_op jit(solution)/shard_map/ppermute | solution.py:26
  102.2 2.7 %shard_map.79 = (f32[256,1024]{1,0:T(8,128)S(1)}, f32[256,1024]{1,0:T(8,128)}, bf16[512,512]{1,0:T(8,128)(2,1)S(1)}) custom-call(s32[1]{0:T(128)} %bitcast.place, bf16[128,512]{1,0:T(8,128)(2,1)S(1)} %fusion.6.g0, bf16[128,512]{1,0:T(8,128)(2,1)S(1)} %collective-permute-done.14.g1, bf16[128,512]{1,0:T(8,128)(2,1)S(1)} %collective-permute-done.15.g2, ...), custom_call_target="tpu_custom_call" | custom-call | tf_op jit(solution)/shard_map/pallas_call | solution.py:50
  107.0 4.9 %all-to-all-start.3 = ((bf16[16,64,512]{2,1,0:T(8,128)(2,1)}), bf16[16,64,512]{2,1,0:T(8,128)(2,1)S(1)}, u32[]{:S(2)}, u32[]{:S(2)}) async-start(bf16[16,64,512]{2,1,0:T(8,128)(2,1)} %bitcast.39), calls=%async_computation.3 | async-start | bytes 2097152 | tf_op jit(solution)/shard_map/all_to_all | solution.py:21
  117.6 2.4 %collective-permute-start.22 = (f16[32,1024]{1,0:T(8,128)(2,1)S(1)}, f16[32,1024]{1,0:T(8,128)(2,1)S(1)}, u32[]{:S(2)}, u32[]{:S(2)}) collective-permute-start(f16[32,1024]{1,0:T(8,128)(2,1)S(1)} %get-tuple-element.57), channel_id=1, source_target_pairs={{0,192},{32,224},{64,128},{96,160},{128,64},{160,96},{192,0},{224,... | collective-permute-start | bytes 196616 | tf_op jit(solution)/shard_map/ppermute | solution.py:36
  122.1 5.8 %collective-permute-done.18 = f16[32,1024]{1,0:T(8,128)(2,1)S(1)} collective-permute-done((f16[32,1024]{1,0:T(8,128)(2,1)S(1)}, f16[32,1024]{1,0:T(8,128)(2,1)S(1)}, u32[]{:S(2)}, u32[]{:S(2)}) %collective-permute-start.18) | collective-permute-done | bytes 65568 | tf_op jit(solution)/shard_map/ppermute | solution.py:36
  129.3 2.6 %collective-permute-start.19 = (f16[32,1024]{1,0:T(8,128)(2,1)S(1)}, f16[32,1024]{1,0:T(8,128)(2,1)S(1)}, u32[]{:S(2)}, u32[]{:S(2)}) collective-permute-start(f16[32,1024]{1,0:T(8,128)(2,1)S(1)} %get-tuple-element.60), channel_id=1, source_target_pairs={{0,96},{32,0},{64,32},{96,64},{128,224},{160,128},{192,160},{224,1... | collective-permute-start | bytes 196616 | tf_op jit(solution)/shard_map/ppermute | solution.py:36
  134.4 2.2 %collective-permute-start.26 = (f32[8,1024]{1,0:T(8,128)S(1)}, f32[8,1024]{1,0:T(8,128)S(1)}, u32[]{:S(2)}, u32[]{:S(2)}) collective-permute-start(f32[8,1024]{1,0:T(8,128)S(1)} %get-tuple-element.62), channel_id=1, source_target_pairs={{0,16},{8,24},{16,0},{24,8},{1,17},{9,25},{17,1},{25,9},{2,18},{10... | collective-permute-start | bytes 98312 | tf_op jit(solution)/shard_map/ppermute | solution.py:26
  142.1 2.2 %collective-permute-start.29 = (f32[8,1024]{1,0:T(8,128)S(1)}, f32[8,1024]{1,0:T(8,128)S(1)}, u32[]{:S(2)}, u32[]{:S(2)}) collective-permute-start(f32[8,1024]{1,0:T(8,128)S(1)} %get-tuple-element.41), channel_id=1, source_target_pairs={{0,2},{1,3},{2,0},{3,1},{4,6},{5,7},{6,4},{7,5},{8,10},{9,11},{10,... | collective-permute-start | bytes 98312 | tf_op jit(solution)/shard_map/ppermute | solution.py:26
  146.1 3.2 %shard_map.81 = f32[64,8192]{1,0:T(8,128)} custom-call(s32[1]{0:T(128)} %bitcast.place, bf16[16,64,512]{2,1,0:T(8,128)(2,1)S(1)} %all-to-all-done.3.dense, bf16[16,8,512]{2,1,0:T(8,128)(2,1)S(1)} %all-to-all-done.1.along), custom_call_target="tpu_custom_call" | custom-call | tf_op jit(solution)/shard_map/pallas_call | solution.py:50
  (104 shorter events, 50.5 us)
Async XLA Ops:
  4.1 38.6 %all-to-all-start = ((bf16[16,80,512]{2,1,0:T(8,128)(2,1)}), bf16[16,80,512]{2,1,0:T(8,128)(2,1)S(1)}, u32[]{:S(2)}, u32[]{:S(2)}) async-start(bf16[16,80,512]{2,1,0:T(8,128)(2,1)} %get-tuple-element.26), calls=%async_computation | async-start | bytes 2621440 | tf_op jit(solution)/shard_map/all_to_all | solution.py:21
  18.7 23.0 %collective-permute-start.9 = (bf16[32,1024]{1,0:T(8,128)(2,1)S(1)}, bf16[32,1024]{1,0:T(8,128)(2,1)S(1)}, u32[]{:S(2)}, u32[]{:S(2)}) collective-permute-start(bf16[32,1024]{1,0:T(8,128)(2,1)S(1)} %pad_maximum_fusion.1), channel_id=1, source_target_pairs={{0,224},{32,128},{64,160},{96,192},{128,96},{160,0},{192,32},{224,... | collective-permute-start | bytes 196616 | tf_op jit(solution)/shard_map/ppermute | solution.py:36
  20.3 21.4 %collective-permute-start.8 = (bf16[32,1024]{1,0:T(8,128)(2,1)S(1)}, bf16[32,1024]{1,0:T(8,128)(2,1)S(1)}, u32[]{:S(2)}, u32[]{:S(2)}) collective-permute-start(bf16[32,1024]{1,0:T(8,128)(2,1)S(1)} %pad_maximum_fusion.1), channel_id=1, source_target_pairs={{0,96},{32,0},{64,32},{96,64},{128,224},{160,128},{192,160},{224,1... | collective-permute-start | bytes 196616 | tf_op jit(solution)/shard_map/ppermute | solution.py:36
  22.9 18.7 %collective-permute-start.7 = (bf16[32,1024]{1,0:T(8,128)(2,1)S(1)}, bf16[32,1024]{1,0:T(8,128)(2,1)S(1)}, u32[]{:S(2)}, u32[]{:S(2)}) collective-permute-start(bf16[32,1024]{1,0:T(8,128)(2,1)S(1)} %pad_maximum_fusion.1), channel_id=1, source_target_pairs={{0,192},{32,224},{64,128},{96,160},{128,64},{160,96},{192,0},{224,... | collective-permute-start | bytes 196616 | tf_op jit(solution)/shard_map/ppermute | solution.py:36
  23.2 18.4 %collective-permute-start.6 = (bf16[32,1024]{1,0:T(8,128)(2,1)S(1)}, bf16[32,1024]{1,0:T(8,128)(2,1)S(1)}, u32[]{:S(2)}, u32[]{:S(2)}) collective-permute-start(bf16[32,1024]{1,0:T(8,128)(2,1)S(1)} %pad_maximum_fusion.1), channel_id=1, source_target_pairs={{0,64},{32,96},{64,0},{96,32},{128,192},{160,224},{192,128},{224,1... | collective-permute-start | bytes 196616 | tf_op jit(solution)/shard_map/ppermute | solution.py:36
  41.7 7.7 %collective-permute-start.10 = (bf16[256,1024]{1,0:T(8,128)(2,1)S(1)}, bf16[256,1024]{1,0:T(8,128)(2,1)S(1)}, u32[]{:S(2)}, u32[]{:S(2)}) collective-permute-start(bf16[256,1024]{1,0:T(8,128)(2,1)S(1)} %constant_dynamic-update-slice_fusion.same), channel_id=1, source_target_pairs={{0,4},{4,0},{1,5},{5,1},{2,6},{6,2},{3,7},{7,3},{8,12},{12,8},{9,1... | collective-permute-start | bytes 1572872 | tf_op jit(solution)/shard_map/ppermute | solution.py:26
  42.7 28.5 %all-to-all-start.1 = ((bf16[16,8,512]{2,1,0:T(8,128)(2,1)}), bf16[16,8,512]{2,1,0:T(8,128)(2,1)S(1)}, u32[]{:S(2)}, u32[]{:S(2)}) async-start(bf16[16,8,512]{2,1,0:T(8,128)(2,1)} %maximum_bitcast_fusion), calls=%async_computation.1 | async-start | bytes 262144 | tf_op jit(solution)/shard_map/all_to_all | solution.py:21
  50.8 14.5 %collective-permute-start.11 = (f32[128,512]{1,0:T(8,128)S(1)}, f32[128,512]{1,0:T(8,128)}, u32[]{:S(2)}, u32[]{:S(2)}) collective-permute-start(f32[128,512]{1,0:T(8,128)S(1)} %get-tuple-element.32), channel_id=1, source_target_pairs={{0,24},{8,0},{16,8},{24,16},{1,25},{9,1},{17,9},{25,17},{2,26},{10... | collective-permute-start | bytes 786440 | tf_op jit(solution)/shard_map/ppermute | solution.py:26
  53.9 11.5 %collective-permute-start.12 = (f32[128,512]{1,0:T(8,128)S(1)}, f32[128,512]{1,0:T(8,128)}, u32[]{:S(2)}, u32[]{:S(2)}) collective-permute-start(f32[128,512]{1,0:T(8,128)S(1)} %get-tuple-element.33), channel_id=1, source_target_pairs={{0,16},{8,24},{16,0},{24,8},{1,17},{9,25},{17,1},{25,9},{2,18},{10... | collective-permute-start | bytes 786440 | tf_op jit(solution)/shard_map/ppermute | solution.py:26
  54.4 14.7 %collective-permute-start.13 = (f32[128,512]{1,0:T(8,128)S(1)}, f32[128,512]{1,0:T(8,128)}, u32[]{:S(2)}, u32[]{:S(2)}) collective-permute-start(f32[128,512]{1,0:T(8,128)S(1)} %get-tuple-element.34), channel_id=1, source_target_pairs={{0,8},{8,16},{16,24},{24,0},{1,9},{9,17},{17,25},{25,1},{2,10},{10... | collective-permute-start | bytes 786440 | tf_op jit(solution)/shard_map/ppermute | solution.py:26
  71.8 19.8 %all-to-all-start.2 = ((f32[64,2,128]{2,1,0:T(2,128)}), f32[64,2,128]{2,1,0:T(2,128)S(1)}, u32[]{:S(2)}, u32[]{:S(2)}) async-start(f32[64,2,128]{2,1,0:T(2,128)} %broadcast_in_dim.4), calls=%async_computation.2 | async-start | bytes 131072 | tf_op jit(solution)/shard_map/all_to_all | solution.py:21
  91.9 6.4 %collective-permute-start.16 = (bf16[128,512]{1,0:T(8,128)(2,1)S(1)}, bf16[128,512]{1,0:T(8,128)(2,1)S(1)}, u32[]{:S(2)}, u32[]{:S(2)}) collective-permute-start(bf16[128,512]{1,0:T(8,128)(2,1)S(1)} %fusion.6.g0), channel_id=1, source_target_pairs={{0,24},{8,0},{16,8},{24,16},{1,25},{9,1},{17,9},{25,17},{2,26},{10... | collective-permute-start | bytes 393224 | tf_op jit(solution)/shard_map/ppermute | solution.py:26
  92.7 7.9 %collective-permute-start.15 = (bf16[128,512]{1,0:T(8,128)(2,1)S(1)}, bf16[128,512]{1,0:T(8,128)(2,1)S(1)}, u32[]{:S(2)}, u32[]{:S(2)}) collective-permute-start(bf16[128,512]{1,0:T(8,128)(2,1)S(1)} %fusion.6.g0), channel_id=1, source_target_pairs={{0,16},{8,24},{16,0},{24,8},{1,17},{9,25},{17,1},{25,9},{2,18},{10... | collective-permute-start | bytes 393224 | tf_op jit(solution)/shard_map/ppermute | solution.py:26
  93.1 9.1 %collective-permute-start.14 = (bf16[128,512]{1,0:T(8,128)(2,1)S(1)}, bf16[128,512]{1,0:T(8,128)(2,1)S(1)}, u32[]{:S(2)}, u32[]{:S(2)}) collective-permute-start(bf16[128,512]{1,0:T(8,128)(2,1)S(1)} %fusion.6.g0), channel_id=1, source_target_pairs={{0,8},{8,16},{16,24},{24,0},{1,9},{9,17},{17,25},{25,1},{2,10},{10... | collective-permute-start | bytes 393224 | tf_op jit(solution)/shard_map/ppermute | solution.py:26
  104.9 6.9 %collective-permute-start.17 = (f32[256,1024]{1,0:T(8,128)}, f32[256,1024]{1,0:T(8,128)}, u32[]{:S(2)}, u32[]{:S(2)}) collective-permute-start(f32[256,1024]{1,0:T(8,128)} %get-tuple-element.38), channel_id=1, source_target_pairs={{0,4},{4,0},{1,5},{5,1},{2,6},{6,2},{3,7},{7,3},{8,12},{12,8},{9,1... | collective-permute-start | bytes 3145736 | tf_op jit(solution)/shard_map/ppermute | solution.py:26
  107.0 39.1 %all-to-all-start.3 = ((bf16[16,64,512]{2,1,0:T(8,128)(2,1)}), bf16[16,64,512]{2,1,0:T(8,128)(2,1)S(1)}, u32[]{:S(2)}, u32[]{:S(2)}) async-start(bf16[16,64,512]{2,1,0:T(8,128)(2,1)} %bitcast.39), calls=%async_computation.3 | async-start | bytes 2097152 | tf_op jit(solution)/shard_map/all_to_all | solution.py:21
  113.4 14.5 %collective-permute-start.18 = (f16[32,1024]{1,0:T(8,128)(2,1)S(1)}, f16[32,1024]{1,0:T(8,128)(2,1)S(1)}, u32[]{:S(2)}, u32[]{:S(2)}) collective-permute-start(f16[32,1024]{1,0:T(8,128)(2,1)S(1)} %get-tuple-element.54), channel_id=1, source_target_pairs={{0,128},{32,160},{64,192},{96,224},{128,0},{160,32},{192,64},{224,... | collective-permute-start | bytes 196616 | tf_op jit(solution)/shard_map/ppermute | solution.py:36
  115.0 14.3 %collective-permute-start.24 = (f16[32,1024]{1,0:T(8,128)(2,1)S(1)}, f16[32,1024]{1,0:T(8,128)(2,1)S(1)}, u32[]{:S(2)}, u32[]{:S(2)}) collective-permute-start(f16[32,1024]{1,0:T(8,128)(2,1)S(1)} %get-tuple-element.55), channel_id=1, source_target_pairs={{0,160},{32,192},{64,224},{96,128},{128,32},{160,64},{192,96},{224... | collective-permute-start | bytes 196616 | tf_op jit(solution)/shard_map/ppermute | solution.py:36
  116.4 15.5 %collective-permute-start.23 = (f16[32,1024]{1,0:T(8,128)(2,1)S(1)}, f16[32,1024]{1,0:T(8,128)(2,1)S(1)}, u32[]{:S(2)}, u32[]{:S(2)}) collective-permute-start(f16[32,1024]{1,0:T(8,128)(2,1)S(1)} %get-tuple-element.56), channel_id=1, source_target_pairs={{0,32},{32,64},{64,96},{96,0},{128,160},{160,192},{192,224},{224,1... | collective-permute-start | bytes 196616 | tf_op jit(solution)/shard_map/ppermute | solution.py:36
  117.6 14.6 %collective-permute-start.22 = (f16[32,1024]{1,0:T(8,128)(2,1)S(1)}, f16[32,1024]{1,0:T(8,128)(2,1)S(1)}, u32[]{:S(2)}, u32[]{:S(2)}) collective-permute-start(f16[32,1024]{1,0:T(8,128)(2,1)S(1)} %get-tuple-element.57), channel_id=1, source_target_pairs={{0,192},{32,224},{64,128},{96,160},{128,64},{160,96},{192,0},{224,... | collective-permute-start | bytes 196616 | tf_op jit(solution)/shard_map/ppermute | solution.py:36
  120.0 12.2 %collective-permute-start.21 = (f16[32,1024]{1,0:T(8,128)(2,1)S(1)}, f16[32,1024]{1,0:T(8,128)(2,1)S(1)}, u32[]{:S(2)}, u32[]{:S(2)}) collective-permute-start(f16[32,1024]{1,0:T(8,128)(2,1)S(1)} %get-tuple-element.58), channel_id=1, source_target_pairs={{0,64},{32,96},{64,0},{96,32},{128,192},{160,224},{192,128},{224,1... | collective-permute-start | bytes 196616 | tf_op jit(solution)/shard_map/ppermute | solution.py:36
  140.8 8.5 %collective-permute-start.28 = (f32[8,1024]{1,0:T(8,128)S(1)}, f32[8,1024]{1,0:T(8,128)S(1)}, u32[]{:S(2)}, u32[]{:S(2)}) collective-permute-start(f32[8,1024]{1,0:T(8,128)S(1)} %get-tuple-element.40), channel_id=1, source_target_pairs={{0,1},{1,2},{2,3},{3,0},{4,5},{5,6},{6,7},{7,4},{8,9},{9,10},{10,1... | collective-permute-start | bytes 98312 | tf_op jit(solution)/shard_map/ppermute | solution.py:26
  142.1 8.0 %collective-permute-start.29 = (f32[8,1024]{1,0:T(8,128)S(1)}, f32[8,1024]{1,0:T(8,128)S(1)}, u32[]{:S(2)}, u32[]{:S(2)}) collective-permute-start(f32[8,1024]{1,0:T(8,128)S(1)} %get-tuple-element.41), channel_id=1, source_target_pairs={{0,2},{1,3},{2,0},{3,1},{4,6},{5,7},{6,4},{7,5},{8,10},{9,11},{10,... | collective-permute-start | bytes 98312 | tf_op jit(solution)/shard_map/ppermute | solution.py:26
  144.3 5.8 %collective-permute-start.30 = (f32[8,1024]{1,0:T(8,128)S(1)}, f32[8,1024]{1,0:T(8,128)S(1)}, u32[]{:S(2)}, u32[]{:S(2)}) collective-permute-start(f32[8,1024]{1,0:T(8,128)S(1)} %get-tuple-element.42), channel_id=1, source_target_pairs={{0,3},{1,0},{2,1},{3,2},{4,7},{5,4},{6,5},{7,6},{8,11},{9,8},{10,9... | collective-permute-start | bytes 98312 | tf_op jit(solution)/shard_map/ppermute | solution.py:26
  (11 other events, 55.3 us)
where the time goes:
time: 153 us; the launch traced here: 151 us
  starting transfers between devices  71.3 us (47%)
  waiting for transfers between devices  52.4 us (34%)
  Pallas kernels  10.8 us (7%)
  local copies, waits for them, and re-layouts  7.18 us (5%)
  other arithmetic  6.29 us (4%)
  matrix products  1.93 us (1%)
    all_to_all x4, starting transfers between devices, exchange(): return lax.all_to_all(x, axes, 0, 0, tiled=True)  28.3 us
    ppermute x17, waiting for transfers between devices, shifted(): return lax.ppermute(x, axis, [(k, (k + step) % size) for k in range(size)])  22.2 us
    ppermute x14, starting transfers between devices, shifted_both(): return lax.ppermute(x, ('z', 'x'), pairs)  21.7 us
    ppermute x14, waiting for transfers between devices, shifted_both(): return lax.ppermute(x, ('z', 'x'), pairs)  21.7 us
    ppermute x17, starting transfers between devices, shifted(): return lax.ppermute(x, axis, [(k, (k + step) % size) for k in range(size)])  21.3 us
    pallas_call x5, Pallas kernels, run(): pl.pallas_call(body, out_shape=[spec.memory_space(out.shape, out.dtype) f...  10.8 us
    all_to_all x4, waiting for transfers between devices, exchange(): return lax.all_to_all(x, axes, 0, 0, tiled=True)  8.43 us
    unnamed x10, local copies, waits for them, and re-layouts  3.69 us
  transfers between devices with their start and end apart: 35, of which 20 were waited for; matrix products, arithmetic and copies ran while one was open for 9% of the time, Pallas kernels for 3%

commit v1 on v0

--- a/solution.py
+++ b/solution.py
@@ -193,30 +193,39 @@
                 ]
 
 
-def head_kernel(place, dense, along, result, mine, out, sems, *, sizes):
-    rows, block = out.shape[0], dense.shape[2]
+def embed_kernel(place, along, out, mine, *, sizes):
+    rows, block = out.shape[0], along.shape[2]
     own = along.shape[1]
     at = 0
     for y in range(block // 128):
-        for j in range(dense.shape[0]):
+        for j in range(along.shape[0]):
             mine[at : at + own, :] = along[j, :, y * 128 : (y + 1) * 128]
             at += own
     numbers = mine[:, rows : rows + 2].astype(jnp.float32)
     ids = (numbers[:, :1] * 256 + numbers[:, 1:]).astype(jnp.int32)
     ids = ids - lax.rem(place[0], sizes[4]) * out.shape[1]
     spots = lax.broadcasted_iota(jnp.int32, (at, block), 1)
-    moves = []
-    for j in range(dense.shape[0]):
+    for j in range(along.shape[0]):
         found = jnp.where(ids - j * block == spots, 1.0, 0.0).astype(jnp.bfloat16)
-        made = lax.dot_general(
+        out[:, j * block : (j + 1) * block] = lax.dot_general(
             mine[:, :rows], found, (((0,), (0,)), ((), ())), preferred_element_type=jnp.float32
         )
-        lanes = slice(j * block, (j + 1) * block)
-        out[:, lanes] = made + dense[j].astype(jnp.float32)
-        moves.append(pltpu.make_async_copy(out.at[:, lanes], result.at[:, lanes], sems.at[j]))
-        moves[j].start()
-    for move in moves:
-        move.wait()
+
+
+def head_kernel(place, looked, *refs):
+    parts, (result, out, sems) = refs[:-3], refs[-3:]
+    width = parts[0].shape[2]
+    saves = []
+    for j in range(parts[0].shape[0]):
+        for k, part in enumerate(parts):
+            at = (j * len(parts) + k) * width
+            lanes = slice(at, at + width)
+            out[:, lanes] = looked[:, lanes] + part[j].astype(jnp.float32)
+        lanes = slice(j * width * len(parts), (j + 1) * width * len(parts))
+        saves.append(pltpu.make_async_copy(out.at[:, lanes], result.at[:, lanes], sems.at[j]))
+        saves[j].start()
+    for save in saves:
+        save.wait()
 
 
 def per_device(hidden, embed_grad, token_ids, loss_weight, teacher_logits, head):
@@ -293,8 +302,11 @@
         [VMEM] * ny + [HBM],
     )(place, *gaps, head_part)
 
-    dense = dot(same, gap_all[:half], ((0,), (0,))) + dot(other, gap_all[half:], ((0,), (0,)))
-    dense = dense.astype(bf16).reshape(cols, rows, block)
+    dense = []
+    for k in range(1):
+        at = gap_all[:, k * block // 1 : (k + 1) * block // 1]
+        made = dot(same, at[:half], ((0,), (0,))) + dot(other, at[half:], ((0,), (0,)))
+        dense.append(made.astype(bf16).reshape(cols, rows, block // 1))
 
     back = back + shifted(back_other, "c", 1)
     back = back.reshape(nx * nz, ny * own, part)
@@ -302,7 +314,12 @@
     came = []
     for k, (dz, dx) in enumerate(steps, 1):
         came.append(shifted_both(sent[k], dz, -dx).astype(f32) * (1 / FIT))
-    dense = exchange(dense, COLS)
+    dense[0] = exchange(dense[0], COLS)
+    looked = call(
+        functools.partial(embed_kernel, sizes=shape),
+        [held((rows, vocab), f32)],
+        [pltpu.VMEM((tokens, 128), bf16)],
+    )(place, along)[0]
     total = functools.reduce(jnp.add, came, back[0])
     total = total.reshape(ny, own, part)
     spread = call(
@@ -310,10 +327,10 @@
     )(place, total[0], *[shifted(total[k], "y", -k) for k in range(1, ny)])
     spread = [spread[0]] + [shifted(spread[k], "vocab", k) for k in range(1, nv)]
     head_grad = call(
-        functools.partial(head_kernel, sizes=shape),
+        head_kernel,
         [stored((rows, vocab), f32)],
-        [pltpu.VMEM((tokens, 128), bf16), pltpu.VMEM((rows, vocab), f32), pltpu.SemaphoreType.DMA((cols,))],
-    )(place, dense, along)[0]
+        [pltpu.VMEM((rows, vocab), f32), pltpu.SemaphoreType.DMA((cols,))],
+    )(place, looked, *dense)[0]
     spread, head_grad = lax.optimization_barrier((spread, head_grad))
     grad_hidden = functools.reduce(jnp.add, spread).astype(bf16)
     return grad_hidden, head_grad

time: 153 us -> 153 us (level)
    pallas_call x5 -> x6, Pallas kernels: 10.8 us -> 11.3 us  [run(): pl.pallas_call(body, out_shape=[spec.memory_space(out.shape, out.dtype) f...]
where the time goes in v1:
time: 153 us; the launch traced here: 151 us
  starting transfers between devices  71.3 us (47%)
  waiting for transfers between devices  51.8 us (34%)
  Pallas kernels  11.3 us (7%)
  local copies, waits for them, and re-layouts  7.18 us (5%)
  other arithmetic  6.29 us (4%)
  matrix products  1.91 us (1%)
    all_to_all x4, starting transfers between devices, exchange(): return lax.all_to_all(x, axes, 0, 0, tiled=True)  28.3 us
    ppermute x14, waiting for transfers between devices, shifted_both(): return lax.ppermute(x, ('z', 'x'), pairs)  21.7 us
    ppermute x14, starting transfers between devices, shifted_both(): return lax.ppermute(x, ('z', 'x'), pairs)  21.7 us
    ppermute x17, waiting for transfers between devices, shifted(): return lax.ppermute(x, axis, [(k, (k + step) % size) for k in range(size)])  21.6 us
    ppermute x17, starting transfers between devices, shifted(): return lax.ppermute(x, axis, [(k, (k + step) % size) for k in range(size)])  21.3 us
    pallas_call x6, Pallas kernels, run(): pl.pallas_call(body, out_shape=[spec.memory_space(out.shape, out.dtype) f...  11.3 us
    all_to_all x4, waiting for transfers between devices, exchange(): return lax.all_to_all(x, axes, 0, 0, tiled=True)  8.43 us
    unnamed x10, local copies, waits for them, and re-layouts  3.69 us
  transfers between devices with their start and end apart: 35, of which 20 were waited for; matrix products, arithmetic and copies ran while one was open for 9% of the time, Pallas kernels for 3%

profile of v1, /device:TPU:2, one launch (start us, length us, event | category | flops | bytes accessed | tf_op | source)
XLA Modules:
  0.0 150.7 jit_solution(1247249502327406179)
XLA Ops:
  0.6 3.4 %shard_map.77 = (bf16[16,80,512]{2,1,0:T(8,128)(2,1)}, bf16[8,2176]{1,0:T(8,128)(2,1)S(1)}, bf16[8,2176]{1,0:T(8,128)(2,1)S(1)}, bf16[8,2176]{1,0:T(8,128)(2,1)S(1)}, bf16[8,2176]{1,0:T(8,128)(2,1)S(1)}) custom-call(s32[1]{0:T(128)} %bitcast.place, s32[8]{0:T(128)} %ids.1, f32[8]{0:T(128)} %weights.1, bf16[8,4096]{1,0:T(8,128)(2,1)} %hidden.1, ...), custom_call_target="tpu_custom_call" | custom-call | tf_op jit(solution)/shard_map/pallas_call | solution.py:50
  4.1 6.2 %all-to-all-start = ((bf16[16,80,512]{2,1,0:T(8,128)(2,1)}), bf16[16,80,512]{2,1,0:T(8,128)(2,1)S(1)}, u32[]{:S(2)}, u32[]{:S(2)}) async-start(bf16[16,80,512]{2,1,0:T(8,128)(2,1)} %get-tuple-element.26), calls=%async_computation | async-start | bytes 2621440 | tf_op jit(solution)/shard_map/all_to_all | solution.py:21
  11.9 2.9 %collective-permute-start.1 = (bf16[8,2176]{1,0:T(8,128)(2,1)S(1)}, bf16[8,2176]{1,0:T(8,128)(2,1)S(1)}, u32[]{:S(2)}, u32[]{:S(2)}) collective-permute-start(bf16[8,2176]{1,0:T(8,128)(2,1)S(1)} %get-tuple-element.29), channel_id=1, source_target_pairs={{0,16},{8,24},{16,0},{24,8},{1,17},{9,25},{17,1},{25,9},{2,18},{10... | collective-permute-start | bytes 104456 | tf_op jit(solution)/shard_map/ppermute | solution.py:26
  20.3 2.7 %collective-permute-start.8 = (bf16[32,1024]{1,0:T(8,128)(2,1)S(1)}, bf16[32,1024]{1,0:T(8,128)(2,1)S(1)}, u32[]{:S(2)}, u32[]{:S(2)}) collective-permute-start(bf16[32,1024]{1,0:T(8,128)(2,1)S(1)} %pad_maximum_fusion.1), channel_id=1, source_target_pairs={{0,96},{32,0},{64,32},{96,64},{128,224},{160,128},{192,160},{224,1... | collective-permute-start | bytes 196616 | tf_op jit(solution)/shard_map/ppermute | solution.py:36
  23.2 3.3 %collective-permute-start.6 = (bf16[32,1024]{1,0:T(8,128)(2,1)S(1)}, bf16[32,1024]{1,0:T(8,128)(2,1)S(1)}, u32[]{:S(2)}, u32[]{:S(2)}) collective-permute-start(bf16[32,1024]{1,0:T(8,128)(2,1)S(1)} %pad_maximum_fusion.1), channel_id=1, source_target_pairs={{0,64},{32,96},{64,0},{96,32},{128,192},{160,224},{192,128},{224,1... | collective-permute-start | bytes 196616 | tf_op jit(solution)/shard_map/ppermute | solution.py:36
  28.2 4.0 %collective-permute-done.3 = bf16[32,1024]{1,0:T(8,128)(2,1)S(1)} collective-permute-done((bf16[32,1024]{1,0:T(8,128)(2,1)S(1)}, bf16[32,1024]{1,0:T(8,128)(2,1)S(1)}, u32[]{:S(2)}, u32[]{:S(2)}) %collective-permute-start.3) | collective-permute-done | bytes 65568 | tf_op jit(solution)/shard_map/ppermute | solution.py:36
  32.8 3.7 %collective-permute-done.4 = bf16[32,1024]{1,0:T(8,128)(2,1)S(1)} collective-permute-done((bf16[32,1024]{1,0:T(8,128)(2,1)S(1)}, bf16[32,1024]{1,0:T(8,128)(2,1)S(1)}, u32[]{:S(2)}, u32[]{:S(2)}) %collective-permute-start.4) | collective-permute-done | bytes 65568 | tf_op jit(solution)/shard_map/ppermute | solution.py:36
  37.0 4.6 %collective-permute-done.5 = bf16[32,1024]{1,0:T(8,128)(2,1)S(1)} collective-permute-done((bf16[32,1024]{1,0:T(8,128)(2,1)S(1)}, bf16[32,1024]{1,0:T(8,128)(2,1)S(1)}, u32[]{:S(2)}, u32[]{:S(2)}) %collective-permute-start.5) | collective-permute-done | bytes 65568 | tf_op jit(solution)/shard_map/ppermute | solution.py:36
  42.7 5.8 %all-to-all-start.1 = ((bf16[16,8,512]{2,1,0:T(8,128)(2,1)}), bf16[16,8,512]{2,1,0:T(8,128)(2,1)S(1)}, u32[]{:S(2)}, u32[]{:S(2)}) async-start(bf16[16,8,512]{2,1,0:T(8,128)(2,1)} %maximum_bitcast_fusion), calls=%async_computation.1 | async-start | bytes 262144 | tf_op jit(solution)/shard_map/all_to_all | solution.py:21
  50.8 3.1 %collective-permute-start.11 = (f32[128,512]{1,0:T(8,128)S(1)}, f32[128,512]{1,0:T(8,128)}, u32[]{:S(2)}, u32[]{:S(2)}) collective-permute-start(f32[128,512]{1,0:T(8,128)S(1)} %get-tuple-element.32), channel_id=1, source_target_pairs={{0,24},{8,0},{16,8},{24,16},{1,25},{9,1},{17,9},{25,17},{2,26},{10... | collective-permute-start | bytes 786440 | tf_op jit(solution)/shard_map/ppermute | solution.py:26
  61.6 3.8 %collective-permute-done.11 = f32[128,512]{1,0:T(8,128)} collective-permute-done((f32[128,512]{1,0:T(8,128)S(1)}, f32[128,512]{1,0:T(8,128)}, u32[]{:S(2)}, u32[]{:S(2)}) %collective-permute-start.11) | collective-permute-done | bytes 262176 | tf_op jit(solution)/shard_map/ppermute | solution.py:26
  65.4 3.7 %collective-permute-done.13 = f32[128,512]{1,0:T(8,128)} collective-permute-done((f32[128,512]{1,0:T(8,128)S(1)}, f32[128,512]{1,0:T(8,128)}, u32[]{:S(2)}, u32[]{:S(2)}) %collective-permute-start.13) | collective-permute-done | bytes 262176 | tf_op jit(solution)/shard_map/ppermute | solution.py:26
  71.8 11.3 %all-to-all-start.2 = ((f32[64,2,128]{2,1,0:T(2,128)}), f32[64,2,128]{2,1,0:T(2,128)S(1)}, u32[]{:S(2)}, u32[]{:S(2)}) async-start(f32[64,2,128]{2,1,0:T(2,128)} %broadcast_in_dim.4), calls=%async_computation.2 | async-start | bytes 131072 | tf_op jit(solution)/shard_map/all_to_all | solution.py:21
  83.2 8.4 %all-to-all-done.2 = f32[64,2,128]{2,1,0:T(2,128)S(1)} async-done(((f32[64,2,128]{2,1,0:T(2,128)}), f32[64,2,128]{2,1,0:T(2,128)S(1)}, u32[]{:S(2)}, u32[]{:S(2)}) %all-to-all-start.2) | async-done | bytes 65568 | tf_op jit(solution)/shard_map/all_to_all | solution.py:21
  94.0 4.3 %collective-permute-done.16.g3 = bf16[128,512]{1,0:T(8,128)(2,1)S(1)} collective-permute-done((bf16[128,512]{1,0:T(8,128)(2,1)S(1)}, bf16[128,512]{1,0:T(8,128)(2,1)S(1)}, u32[]{:S(2)}, u32[]{:S(2)}) %collective-permute-start.16) | collective-permute-done | bytes 131104 | tf_op jit(solution)/shard_map/ppermute | solution.py:26
  98.3 2.2 %collective-permute-done.15.g2 = bf16[128,512]{1,0:T(8,128)(2,1)S(1)} collective-permute-done((bf16[128,512]{1,0:T(8,128)(2,1)S(1)}, bf16[128,512]{1,0:T(8,128)(2,1)S(1)}, u32[]{:S(2)}, u32[]{:S(2)}) %collective-permute-start.15) | collective-permute-done | bytes 131104 | tf_op jit(solution)/shard_map/ppermute | solution.py:26
  102.2 2.7 %shard_map.79 = (f32[256,1024]{1,0:T(8,128)S(1)}, f32[256,1024]{1,0:T(8,128)}, bf16[512,512]{1,0:T(8,128)(2,1)S(1)}) custom-call(s32[1]{0:T(128)} %bitcast.place, bf16[128,512]{1,0:T(8,128)(2,1)S(1)} %fusion.6.g0, bf16[128,512]{1,0:T(8,128)(2,1)S(1)} %collective-permute-done.14.g1, bf16[128,512]{1,0:T(8,128)(2,1)S(1)} %collective-permute-done.15.g2, ...), custom_call_target="tpu_custom_call" | custom-call | tf_op jit(solution)/shard_map/pallas_call | solution.py:50
  106.9 4.9 %all-to-all-start.3 = ((bf16[16,64,512]{2,1,0:T(8,128)(2,1)}), bf16[16,64,512]{2,1,0:T(8,128)(2,1)S(1)}, u32[]{:S(2)}, u32[]{:S(2)}) async-start(bf16[16,64,512]{2,1,0:T(8,128)(2,1)} %bitcast.39), calls=%async_computation.3 | async-start | bytes 2097152 | tf_op jit(solution)/shard_map/all_to_all | solution.py:21
  117.5 2.4 %collective-permute-start.22 = (f16[32,1024]{1,0:T(8,128)(2,1)S(1)}, f16[32,1024]{1,0:T(8,128)(2,1)S(1)}, u32[]{:S(2)}, u32[]{:S(2)}) collective-permute-start(f16[32,1024]{1,0:T(8,128)(2,1)S(1)} %get-tuple-element.57), channel_id=1, source_target_pairs={{0,192},{32,224},{64,128},{96,160},{128,64},{160,96},{192,0},{224,... | collective-permute-start | bytes 196616 | tf_op jit(solution)/shard_map/ppermute | solution.py:36
  122.0 5.8 %collective-permute-done.18 = f16[32,1024]{1,0:T(8,128)(2,1)S(1)} collective-permute-done((f16[32,1024]{1,0:T(8,128)(2,1)S(1)}, f16[32,1024]{1,0:T(8,128)(2,1)S(1)}, u32[]{:S(2)}, u32[]{:S(2)}) %collective-permute-start.18) | collective-permute-done | bytes 65568 | tf_op jit(solution)/shard_map/ppermute | solution.py:36
  129.3 2.6 %collective-permute-start.19 = (f16[32,1024]{1,0:T(8,128)(2,1)S(1)}, f16[32,1024]{1,0:T(8,128)(2,1)S(1)}, u32[]{:S(2)}, u32[]{:S(2)}) collective-permute-start(f16[32,1024]{1,0:T(8,128)(2,1)S(1)} %get-tuple-element.60), channel_id=1, source_target_pairs={{0,96},{32,0},{64,32},{96,64},{128,224},{160,128},{192,160},{224,1... | collective-permute-start | bytes 196616 | tf_op jit(solution)/shard_map/ppermute | solution.py:36
  134.4 2.2 %collective-permute-start.26 = (f32[8,1024]{1,0:T(8,128)S(1)}, f32[8,1024]{1,0:T(8,128)S(1)}, u32[]{:S(2)}, u32[]{:S(2)}) collective-permute-start(f32[8,1024]{1,0:T(8,128)S(1)} %get-tuple-element.62), channel_id=1, source_target_pairs={{0,16},{8,24},{16,0},{24,8},{1,17},{9,25},{17,1},{25,9},{2,18},{10... | collective-permute-start | bytes 98312 | tf_op jit(solution)/shard_map/ppermute | solution.py:26
  142.1 2.2 %collective-permute-start.29 = (f32[8,1024]{1,0:T(8,128)S(1)}, f32[8,1024]{1,0:T(8,128)S(1)}, u32[]{:S(2)}, u32[]{:S(2)}) collective-permute-start(f32[8,1024]{1,0:T(8,128)S(1)} %get-tuple-element.41), channel_id=1, source_target_pairs={{0,2},{1,3},{2,0},{3,1},{4,6},{5,7},{6,4},{7,5},{8,10},{9,11},{10,... | collective-permute-start | bytes 98312 | tf_op jit(solution)/shard_map/ppermute | solution.py:26
  146.1 2.3 %shard_map.81.looked = f32[64,8192]{1,0:T(8,128)S(1)} custom-call(s32[1]{0:T(128)} %bitcast.place, bf16[16,8,512]{2,1,0:T(8,128)(2,1)S(1)} %all-to-all-done.1.along), custom_call_target="tpu_custom_call" | custom-call | tf_op jit(solution)/shard_map/pallas_call | solution.py:50
  (105 shorter events, 51.3 us)
Async XLA Ops:
  4.1 38.6 %all-to-all-start = ((bf16[16,80,512]{2,1,0:T(8,128)(2,1)}), bf16[16,80,512]{2,1,0:T(8,128)(2,1)S(1)}, u32[]{:S(2)}, u32[]{:S(2)}) async-start(bf16[16,80,512]{2,1,0:T(8,128)(2,1)} %get-tuple-element.26), calls=%async_computation | async-start | bytes 2621440 | tf_op jit(solution)/shard_map/all_to_all | solution.py:21
  18.7 23.0 %collective-permute-start.9 = (bf16[32,1024]{1,0:T(8,128)(2,1)S(1)}, bf16[32,1024]{1,0:T(8,128)(2,1)S(1)}, u32[]{:S(2)}, u32[]{:S(2)}) collective-permute-start(bf16[32,1024]{1,0:T(8,128)(2,1)S(1)} %pad_maximum_fusion.1), channel_id=1, source_target_pairs={{0,224},{32,128},{64,160},{96,192},{128,96},{160,0},{192,32},{224,... | collective-permute-start | bytes 196616 | tf_op jit(solution)/shard_map/ppermute | solution.py:36
  20.3 21.4 %collective-permute-start.8 = (bf16[32,1024]{1,0:T(8,128)(2,1)S(1)}, bf16[32,1024]{1,0:T(8,128)(2,1)S(1)}, u32[]{:S(2)}, u32[]{:S(2)}) collective-permute-start(bf16[32,1024]{1,0:T(8,128)(2,1)S(1)} %pad_maximum_fusion.1), channel_id=1, source_target_pairs={{0,96},{32,0},{64,32},{96,64},{128,224},{160,128},{192,160},{224,1... | collective-permute-start | bytes 196616 | tf_op jit(solution)/shard_map/ppermute | solution.py:36
  22.9 18.7 %collective-permute-start.7 = (bf16[32,1024]{1,0:T(8,128)(2,1)S(1)}, bf16[32,1024]{1,0:T(8,128)(2,1)S(1)}, u32[]{:S(2)}, u32[]{:S(2)}) collective-permute-start(bf16[32,1024]{1,0:T(8,128)(2,1)S(1)} %pad_maximum_fusion.1), channel_id=1, source_target_pairs={{0,192},{32,224},{64,128},{96,160},{128,64},{160,96},{192,0},{224,... | collective-permute-start | bytes 196616 | tf_op jit(solution)/shard_map/ppermute | solution.py:36
  23.2 18.4 %collective-permute-start.6 = (bf16[32,1024]{1,0:T(8,128)(2,1)S(1)}, bf16[32,1024]{1,0:T(8,128)(2,1)S(1)}, u32[]{:S(2)}, u32[]{:S(2)}) collective-permute-start(bf16[32,1024]{1,0:T(8,128)(2,1)S(1)} %pad_maximum_fusion.1), channel_id=1, source_target_pairs={{0,64},{32,96},{64,0},{96,32},{128,192},{160,224},{192,128},{224,1... | collective-permute-start | bytes 196616 | tf_op jit(solution)/shard_map/ppermute | solution.py:36
  41.7 7.7 %collective-permute-start.10 = (bf16[256,1024]{1,0:T(8,128)(2,1)S(1)}, bf16[256,1024]{1,0:T(8,128)(2,1)S(1)}, u32[]{:S(2)}, u32[]{:S(2)}) collective-permute-start(bf16[256,1024]{1,0:T(8,128)(2,1)S(1)} %constant_dynamic-update-slice_fusion.same), channel_id=1, source_target_pairs={{0,4},{4,0},{1,5},{5,1},{2,6},{6,2},{3,7},{7,3},{8,12},{12,8},{9,1... | collective-permute-start | bytes 1572872 | tf_op jit(solution)/shard_map/ppermute | solution.py:26
  42.7 28.5 %all-to-all-start.1 = ((bf16[16,8,512]{2,1,0:T(8,128)(2,1)}), bf16[16,8,512]{2,1,0:T(8,128)(2,1)S(1)}, u32[]{:S(2)}, u32[]{:S(2)}) async-start(bf16[16,8,512]{2,1,0:T(8,128)(2,1)} %maximum_bitcast_fusion), calls=%async_computation.1 | async-start | bytes 262144 | tf_op jit(solution)/shard_map/all_to_all | solution.py:21
  50.8 14.5 %collective-permute-start.11 = (f32[128,512]{1,0:T(8,128)S(1)}, f32[128,512]{1,0:T(8,128)}, u32[]{:S(2)}, u32[]{:S(2)}) collective-permute-start(f32[128,512]{1,0:T(8,128)S(1)} %get-tuple-element.32), channel_id=1, source_target_pairs={{0,24},{8,0},{16,8},{24,16},{1,25},{9,1},{17,9},{25,17},{2,26},{10... | collective-permute-start | bytes 786440 | tf_op jit(solution)/shard_map/ppermute | solution.py:26
  53.9 11.5 %collective-permute-start.12 = (f32[128,512]{1,0:T(8,128)S(1)}, f32[128,512]{1,0:T(8,128)}, u32[]{:S(2)}, u32[]{:S(2)}) collective-permute-start(f32[128,512]{1,0:T(8,128)S(1)} %get-tuple-element.33), channel_id=1, source_target_pairs={{0,16},{8,24},{16,0},{24,8},{1,17},{9,25},{17,1},{25,9},{2,18},{10... | collective-permute-start | bytes 786440 | tf_op jit(solution)/shard_map/ppermute | solution.py:26
  54.4 14.7 %collective-permute-start.13 = (f32[128,512]{1,0:T(8,128)S(1)}, f32[128,512]{1,0:T(8,128)}, u32[]{:S(2)}, u32[]{:S(2)}) collective-permute-start(f32[128,512]{1,0:T(8,128)S(1)} %get-tuple-element.34), channel_id=1, source_target_pairs={{0,8},{8,16},{16,24},{24,0},{1,9},{9,17},{17,25},{25,1},{2,10},{10... | collective-permute-start | bytes 786440 | tf_op jit(solution)/shard_map/ppermute | solution.py:26
  71.8 19.8 %all-to-all-start.2 = ((f32[64,2,128]{2,1,0:T(2,128)}), f32[64,2,128]{2,1,0:T(2,128)S(1)}, u32[]{:S(2)}, u32[]{:S(2)}) async-start(f32[64,2,128]{2,1,0:T(2,128)} %broadcast_in_dim.4), calls=%async_computation.2 | async-start | bytes 131072 | tf_op jit(solution)/shard_map/all_to_all | solution.py:21
  91.9 6.4 %collective-permute-start.16 = (bf16[128,512]{1,0:T(8,128)(2,1)S(1)}, bf16[128,512]{1,0:T(8,128)(2,1)S(1)}, u32[]{:S(2)}, u32[]{:S(2)}) collective-permute-start(bf16[128,512]{1,0:T(8,128)(2,1)S(1)} %fusion.6.g0), channel_id=1, source_target_pairs={{0,24},{8,0},{16,8},{24,16},{1,25},{9,1},{17,9},{25,17},{2,26},{10... | collective-permute-start | bytes 393224 | tf_op jit(solution)/shard_map/ppermute | solution.py:26
  92.7 7.9 %collective-permute-start.15 = (bf16[128,512]{1,0:T(8,128)(2,1)S(1)}, bf16[128,512]{1,0:T(8,128)(2,1)S(1)}, u32[]{:S(2)}, u32[]{:S(2)}) collective-permute-start(bf16[128,512]{1,0:T(8,128)(2,1)S(1)} %fusion.6.g0), channel_id=1, source_target_pairs={{0,16},{8,24},{16,0},{24,8},{1,17},{9,25},{17,1},{25,9},{2,18},{10... | collective-permute-start | bytes 393224 | tf_op jit(solution)/shard_map/ppermute | solution.py:26
  93.1 9.1 %collective-permute-start.14 = (bf16[128,512]{1,0:T(8,128)(2,1)S(1)}, bf16[128,512]{1,0:T(8,128)(2,1)S(1)}, u32[]{:S(2)}, u32[]{:S(2)}) collective-permute-start(bf16[128,512]{1,0:T(8,128)(2,1)S(1)} %fusion.6.g0), channel_id=1, source_target_pairs={{0,8},{8,16},{16,24},{24,0},{1,9},{9,17},{17,25},{25,1},{2,10},{10... | collective-permute-start | bytes 393224 | tf_op jit(solution)/shard_map/ppermute | solution.py:26
  104.9 6.9 %collective-permute-start.17 = (f32[256,1024]{1,0:T(8,128)}, f32[256,1024]{1,0:T(8,128)}, u32[]{:S(2)}, u32[]{:S(2)}) collective-permute-start(f32[256,1024]{1,0:T(8,128)} %get-tuple-element.38), channel_id=1, source_target_pairs={{0,4},{4,0},{1,5},{5,1},{2,6},{6,2},{3,7},{7,3},{8,12},{12,8},{9,1... | collective-permute-start | bytes 3145736 | tf_op jit(solution)/shard_map/ppermute | solution.py:26
  106.9 41.4 %all-to-all-start.3 = ((bf16[16,64,512]{2,1,0:T(8,128)(2,1)}), bf16[16,64,512]{2,1,0:T(8,128)(2,1)S(1)}, u32[]{:S(2)}, u32[]{:S(2)}) async-start(bf16[16,64,512]{2,1,0:T(8,128)(2,1)} %bitcast.39), calls=%async_computation.3 | async-start | bytes 2097152 | tf_op jit(solution)/shard_map/all_to_all | solution.py:21
  113.3 14.5 %collective-permute-start.18 = (f16[32,1024]{1,0:T(8,128)(2,1)S(1)}, f16[32,1024]{1,0:T(8,128)(2,1)S(1)}, u32[]{:S(2)}, u32[]{:S(2)}) collective-permute-start(f16[32,1024]{1,0:T(8,128)(2,1)S(1)} %get-tuple-element.54), channel_id=1, source_target_pairs={{0,128},{32,160},{64,192},{96,224},{128,0},{160,32},{192,64},{224,... | collective-permute-start | bytes 196616 | tf_op jit(solution)/shard_map/ppermute | solution.py:36
  114.9 14.3 %collective-permute-start.24 = (f16[32,1024]{1,0:T(8,128)(2,1)S(1)}, f16[32,1024]{1,0:T(8,128)(2,1)S(1)}, u32[]{:S(2)}, u32[]{:S(2)}) collective-permute-start(f16[32,1024]{1,0:T(8,128)(2,1)S(1)} %get-tuple-element.55), channel_id=1, source_target_pairs={{0,160},{32,192},{64,224},{96,128},{128,32},{160,64},{192,96},{224... | collective-permute-start | bytes 196616 | tf_op jit(solution)/shard_map/ppermute | solution.py:36
  116.4 15.5 %collective-permute-start.23 = (f16[32,1024]{1,0:T(8,128)(2,1)S(1)}, f16[32,1024]{1,0:T(8,128)(2,1)S(1)}, u32[]{:S(2)}, u32[]{:S(2)}) collective-permute-start(f16[32,1024]{1,0:T(8,128)(2,1)S(1)} %get-tuple-element.56), channel_id=1, source_target_pairs={{0,32},{32,64},{64,96},{96,0},{128,160},{160,192},{192,224},{224,1... | collective-permute-start | bytes 196616 | tf_op jit(solution)/shard_map/ppermute | solution.py:36
  117.5 14.6 %collective-permute-start.22 = (f16[32,1024]{1,0:T(8,128)(2,1)S(1)}, f16[32,1024]{1,0:T(8,128)(2,1)S(1)}, u32[]{:S(2)}, u32[]{:S(2)}) collective-permute-start(f16[32,1024]{1,0:T(8,128)(2,1)S(1)} %get-tuple-element.57), channel_id=1, source_target_pairs={{0,192},{32,224},{64,128},{96,160},{128,64},{160,96},{192,0},{224,... | collective-permute-start | bytes 196616 | tf_op jit(solution)/shard_map/ppermute | solution.py:36
  119.9 12.2 %collective-permute-start.21 = (f16[32,1024]{1,0:T(8,128)(2,1)S(1)}, f16[32,1024]{1,0:T(8,128)(2,1)S(1)}, u32[]{:S(2)}, u32[]{:S(2)}) collective-permute-start(f16[32,1024]{1,0:T(8,128)(2,1)S(1)} %get-tuple-element.58), channel_id=1, source_target_pairs={{0,64},{32,96},{64,0},{96,32},{128,192},{160,224},{192,128},{224,1... | collective-permute-start | bytes 196616 | tf_op jit(solution)/shard_map/ppermute | solution.py:36
  140.7 9.1 %collective-permute-start.28 = (f32[8,1024]{1,0:T(8,128)S(1)}, f32[8,1024]{1,0:T(8,128)S(1)}, u32[]{:S(2)}, u32[]{:S(2)}) collective-permute-start(f32[8,1024]{1,0:T(8,128)S(1)} %get-tuple-element.40), channel_id=1, source_target_pairs={{0,1},{1,2},{2,3},{3,0},{4,5},{5,6},{6,7},{7,4},{8,9},{9,10},{10,1... | collective-permute-start | bytes 98312 | tf_op jit(solution)/shard_map/ppermute | solution.py:26
  142.1 8.0 %collective-permute-start.29 = (f32[8,1024]{1,0:T(8,128)S(1)}, f32[8,1024]{1,0:T(8,128)S(1)}, u32[]{:S(2)}, u32[]{:S(2)}) collective-permute-start(f32[8,1024]{1,0:T(8,128)S(1)} %get-tuple-element.41), channel_id=1, source_target_pairs={{0,2},{1,3},{2,0},{3,1},{4,6},{5,7},{6,4},{7,5},{8,10},{9,11},{10,... | collective-permute-start | bytes 98312 | tf_op jit(solution)/shard_map/ppermute | solution.py:26
  144.3 5.8 %collective-permute-start.30 = (f32[8,1024]{1,0:T(8,128)S(1)}, f32[8,1024]{1,0:T(8,128)S(1)}, u32[]{:S(2)}, u32[]{:S(2)}) collective-permute-start(f32[8,1024]{1,0:T(8,128)S(1)} %get-tuple-element.42), channel_id=1, source_target_pairs={{0,3},{1,0},{2,1},{3,2},{4,7},{5,4},{6,5},{7,6},{8,11},{9,8},{10,9... | collective-permute-start | bytes 98312 | tf_op jit(solution)/shard_map/ppermute | solution.py:26
  (11 other events, 55.3 us)

commit v2 on v1

--- a/solution.py
+++ b/solution.py
@@ -91,8 +91,8 @@
 
 def send_kernel(place, ids, weights, hidden, embed, head, teacher, *refs, sizes):
     nz, nx, ny, _, _ = sizes
-    stacked, outs = refs[0], refs[1 : 1 + ny]
-    hidden_here, embed_here, sems = refs[1 + ny :]
+    sent, outs = refs[0], refs[1 : 1 + ny]
+    hidden_here, embed_here, stacked, sems = refs[1 + ny :]
     _, _, y, _ = position(place, sizes)
     rows, own = head.shape[0], teacher.shape[0]
     cols, _, block = stacked.shape
@@ -120,6 +120,14 @@
         weight = weight - piece.astype(jnp.float32)
         for j in range(cols):
             stacked[j, rows + own :, q * 128 : (q + 1) * 128] = piece
+    saves = []
+    for j in range(cols):
+        moves[2 + 2 * j].wait()
+        moves[3 + 2 * j].wait()
+        saves.append(
+            pltpu.make_async_copy(stacked.at[j], sent.at[j], sems.at[2 + 2 * cols + j])
+        )
+        saves[j].start()
     moves[0].wait()
     moves[1].wait()
     for k, out in enumerate(outs):
@@ -129,8 +137,8 @@
             out[:, g * step : (g + 1) * step] = hidden_here[:, lanes]
             out[:, (nz * nx + g) * step : (nz * nx + g + 1) * step] = embed_here[:, lanes]
         out[:, 2 * nz * nx * step :] = number
-    for move in moves[2:]:
-        move.wait()
+    for save in saves:
+        save.wait()
 
 
 def student_kernel(place, same, other, stacked, *refs, sizes, own, rows):
@@ -243,8 +251,12 @@
 
     stacked, *pieces = call(
         functools.partial(send_kernel, sizes=shape),
-        [held((cols, rows + 2 * own, block), bf16)] + [held((own, 2 * part + 128), bf16)] * ny,
-        [pltpu.VMEM((own, width), bf16)] * 2 + [pltpu.SemaphoreType.DMA((2 + 2 * cols,))],
+        [stored((cols, rows + 2 * own, block), bf16)] + [held((own, 2 * part + 128), bf16)] * ny,
+        [pltpu.VMEM((own, width), bf16)] * 2
+        + [
+            pltpu.VMEM((cols, rows + 2 * own, block), bf16),
+            pltpu.SemaphoreType.DMA((2 + 3 * cols,)),
+        ],
         [SMEM, SMEM, HBM, HBM, HBM, HBM],
     )(place, token_ids, loss_weight, hidden, embed_grad, head, teacher_logits)
     stacked = exchange(stacked, COLS)

time: 153 us -> 153 us (level)
  no operation moved by 1% of the time
where the time goes in v2:
time: 153 us; the launch traced here: 150 us
  starting transfers between devices  71.3 us (47%)
  waiting for transfers between devices  51.8 us (34%)
  Pallas kernels  11 us (7%)
  local copies, waits for them, and re-layouts  7.18 us (5%)
  other arithmetic  6.29 us (4%)
  matrix products  1.91 us (1%)
    all_to_all x4, starting transfers between devices, exchange(): return lax.all_to_all(x, axes, 0, 0, tiled=True)  28.3 us
    ppermute x14, starting transfers between devices, shifted_both(): return lax.ppermute(x, ('z', 'x'), pairs)  21.7 us
    ppermute x14, waiting for transfers between devices, shifted_both(): return lax.ppermute(x, ('z', 'x'), pairs)  21.7 us
    ppermute x17, waiting for transfers between devices, shifted(): return lax.ppermute(x, axis, [(k, (k + step) % size) for k in range(size)])  21.6 us
    ppermute x17, starting transfers between devices, shifted(): return lax.ppermute(x, axis, [(k, (k + step) % size) for k in range(size)])  21.3 us
    pallas_call x6, Pallas kernels, run(): pl.pallas_call(body, out_shape=[spec.memory_space(out.shape, out.dtype) f...  11 us
    all_to_all x4, waiting for transfers between devices, exchange(): return lax.all_to_all(x, axes, 0, 0, tiled=True)  8.43 us
    unnamed x10, local copies, waits for them, and re-layouts  3.69 us
  transfers between devices with their start and end apart: 35, of which 20 were waited for; matrix products, arithmetic and copies ran while one was open for 9% of the time, Pallas kernels for 3%

profile of v2, /device:TPU:2, one launch (start us, length us, event | category | flops | bytes accessed | tf_op | source)
XLA Modules:
  0.0 150.5 jit_solution(4745396972280446565)
XLA Ops:
  0.6 3.2 %shard_map.77 = (bf16[16,80,512]{2,1,0:T(8,128)(2,1)}, bf16[8,2176]{1,0:T(8,128)(2,1)S(1)}, bf16[8,2176]{1,0:T(8,128)(2,1)S(1)}, bf16[8,2176]{1,0:T(8,128)(2,1)S(1)}, bf16[8,2176]{1,0:T(8,128)(2,1)S(1)}) custom-call(s32[1]{0:T(128)} %bitcast.place, s32[8]{0:T(128)} %ids.1, f32[8]{0:T(128)} %weights.1, bf16[8,4096]{1,0:T(8,128)(2,1)} %hidden.1, ...), custom_call_target="tpu_custom_call" | custom-call | tf_op jit(solution)/shard_map/pallas_call | solution.py:50
  3.8 6.2 %all-to-all-start = ((bf16[16,80,512]{2,1,0:T(8,128)(2,1)}), bf16[16,80,512]{2,1,0:T(8,128)(2,1)S(1)}, u32[]{:S(2)}, u32[]{:S(2)}) async-start(bf16[16,80,512]{2,1,0:T(8,128)(2,1)} %get-tuple-element.26), calls=%async_computation | async-start | bytes 2621440 | tf_op jit(solution)/shard_map/all_to_all | solution.py:21
  11.6 2.9 %collective-permute-start.1 = (bf16[8,2176]{1,0:T(8,128)(2,1)S(1)}, bf16[8,2176]{1,0:T(8,128)(2,1)S(1)}, u32[]{:S(2)}, u32[]{:S(2)}) collective-permute-start(bf16[8,2176]{1,0:T(8,128)(2,1)S(1)} %get-tuple-element.29), channel_id=1, source_target_pairs={{0,16},{8,24},{16,0},{24,8},{1,17},{9,25},{17,1},{25,9},{2,18},{10... | collective-permute-start | bytes 104456 | tf_op jit(solution)/shard_map/ppermute | solution.py:26
  20.0 2.7 %collective-permute-start.8 = (bf16[32,1024]{1,0:T(8,128)(2,1)S(1)}, bf16[32,1024]{1,0:T(8,128)(2,1)S(1)}, u32[]{:S(2)}, u32[]{:S(2)}) collective-permute-start(bf16[32,1024]{1,0:T(8,128)(2,1)S(1)} %pad_maximum_fusion.1), channel_id=1, source_target_pairs={{0,96},{32,0},{64,32},{96,64},{128,224},{160,128},{192,160},{224,1... | collective-permute-start | bytes 196616 | tf_op jit(solution)/shard_map/ppermute | solution.py:36
  22.9 3.3 %collective-permute-start.6 = (bf16[32,1024]{1,0:T(8,128)(2,1)S(1)}, bf16[32,1024]{1,0:T(8,128)(2,1)S(1)}, u32[]{:S(2)}, u32[]{:S(2)}) collective-permute-start(bf16[32,1024]{1,0:T(8,128)(2,1)S(1)} %pad_maximum_fusion.1), channel_id=1, source_target_pairs={{0,64},{32,96},{64,0},{96,32},{128,192},{160,224},{192,128},{224,1... | collective-permute-start | bytes 196616 | tf_op jit(solution)/shard_map/ppermute | solution.py:36
  27.9 4.0 %collective-permute-done.3 = bf16[32,1024]{1,0:T(8,128)(2,1)S(1)} collective-permute-done((bf16[32,1024]{1,0:T(8,128)(2,1)S(1)}, bf16[32,1024]{1,0:T(8,128)(2,1)S(1)}, u32[]{:S(2)}, u32[]{:S(2)}) %collective-permute-start.3) | collective-permute-done | bytes 65568 | tf_op jit(solution)/shard_map/ppermute | solution.py:36
  32.5 3.7 %collective-permute-done.4 = bf16[32,1024]{1,0:T(8,128)(2,1)S(1)} collective-permute-done((bf16[32,1024]{1,0:T(8,128)(2,1)S(1)}, bf16[32,1024]{1,0:T(8,128)(2,1)S(1)}, u32[]{:S(2)}, u32[]{:S(2)}) %collective-permute-start.4) | collective-permute-done | bytes 65568 | tf_op jit(solution)/shard_map/ppermute | solution.py:36
  36.8 4.6 %collective-permute-done.5 = bf16[32,1024]{1,0:T(8,128)(2,1)S(1)} collective-permute-done((bf16[32,1024]{1,0:T(8,128)(2,1)S(1)}, bf16[32,1024]{1,0:T(8,128)(2,1)S(1)}, u32[]{:S(2)}, u32[]{:S(2)}) %collective-permute-start.5) | collective-permute-done | bytes 65568 | tf_op jit(solution)/shard_map/ppermute | solution.py:36
  42.4 5.8 %all-to-all-start.1 = ((bf16[16,8,512]{2,1,0:T(8,128)(2,1)}), bf16[16,8,512]{2,1,0:T(8,128)(2,1)S(1)}, u32[]{:S(2)}, u32[]{:S(2)}) async-start(bf16[16,8,512]{2,1,0:T(8,128)(2,1)} %maximum_bitcast_fusion), calls=%async_computation.1 | async-start | bytes 262144 | tf_op jit(solution)/shard_map/all_to_all | solution.py:21
  50.6 3.1 %collective-permute-start.11 = (f32[128,512]{1,0:T(8,128)S(1)}, f32[128,512]{1,0:T(8,128)}, u32[]{:S(2)}, u32[]{:S(2)}) collective-permute-start(f32[128,512]{1,0:T(8,128)S(1)} %get-tuple-element.32), channel_id=1, source_target_pairs={{0,24},{8,0},{16,8},{24,16},{1,25},{9,1},{17,9},{25,17},{2,26},{10... | collective-permute-start | bytes 786440 | tf_op jit(solution)/shard_map/ppermute | solution.py:26
  61.3 3.8 %collective-permute-done.11 = f32[128,512]{1,0:T(8,128)} collective-permute-done((f32[128,512]{1,0:T(8,128)S(1)}, f32[128,512]{1,0:T(8,128)}, u32[]{:S(2)}, u32[]{:S(2)}) %collective-permute-start.11) | collective-permute-done | bytes 262176 | tf_op jit(solution)/shard_map/ppermute | solution.py:26
  65.1 3.7 %collective-permute-done.13 = f32[128,512]{1,0:T(8,128)} collective-permute-done((f32[128,512]{1,0:T(8,128)S(1)}, f32[128,512]{1,0:T(8,128)}, u32[]{:S(2)}, u32[]{:S(2)}) %collective-permute-start.13) | collective-permute-done | bytes 262176 | tf_op jit(solution)/shard_map/ppermute | solution.py:26
  71.5 11.3 %all-to-all-start.2 = ((f32[64,2,128]{2,1,0:T(2,128)}), f32[64,2,128]{2,1,0:T(2,128)S(1)}, u32[]{:S(2)}, u32[]{:S(2)}) async-start(f32[64,2,128]{2,1,0:T(2,128)} %broadcast_in_dim.4), calls=%async_computation.2 | async-start | bytes 131072 | tf_op jit(solution)/shard_map/all_to_all | solution.py:21
  82.9 8.4 %all-to-all-done.2 = f32[64,2,128]{2,1,0:T(2,128)S(1)} async-done(((f32[64,2,128]{2,1,0:T(2,128)}), f32[64,2,128]{2,1,0:T(2,128)S(1)}, u32[]{:S(2)}, u32[]{:S(2)}) %all-to-all-start.2) | async-done | bytes 65568 | tf_op jit(solution)/shard_map/all_to_all | solution.py:21
  93.7 4.3 %collective-permute-done.16.g3 = bf16[128,512]{1,0:T(8,128)(2,1)S(1)} collective-permute-done((bf16[128,512]{1,0:T(8,128)(2,1)S(1)}, bf16[128,512]{1,0:T(8,128)(2,1)S(1)}, u32[]{:S(2)}, u32[]{:S(2)}) %collective-permute-start.16) | collective-permute-done | bytes 131104 | tf_op jit(solution)/shard_map/ppermute | solution.py:26
  98.1 2.2 %collective-permute-done.15.g2 = bf16[128,512]{1,0:T(8,128)(2,1)S(1)} collective-permute-done((bf16[128,512]{1,0:T(8,128)(2,1)S(1)}, bf16[128,512]{1,0:T(8,128)(2,1)S(1)}, u32[]{:S(2)}, u32[]{:S(2)}) %collective-permute-start.15) | collective-permute-done | bytes 131104 | tf_op jit(solution)/shard_map/ppermute | solution.py:26
  102.0 2.7 %shard_map.79 = (f32[256,1024]{1,0:T(8,128)S(1)}, f32[256,1024]{1,0:T(8,128)}, bf16[512,512]{1,0:T(8,128)(2,1)S(1)}) custom-call(s32[1]{0:T(128)} %bitcast.place, bf16[128,512]{1,0:T(8,128)(2,1)S(1)} %fusion.6.g0, bf16[128,512]{1,0:T(8,128)(2,1)S(1)} %collective-permute-done.14.g1, bf16[128,512]{1,0:T(8,128)(2,1)S(1)} %collective-permute-done.15.g2, ...), custom_call_target="tpu_custom_call" | custom-call | tf_op jit(solution)/shard_map/pallas_call | solution.py:50
  106.7 4.9 %all-to-all-start.3 = ((bf16[16,64,512]{2,1,0:T(8,128)(2,1)}), bf16[16,64,512]{2,1,0:T(8,128)(2,1)S(1)}, u32[]{:S(2)}, u32[]{:S(2)}) async-start(bf16[16,64,512]{2,1,0:T(8,128)(2,1)} %bitcast.39), calls=%async_computation.3 | async-start | bytes 2097152 | tf_op jit(solution)/shard_map/all_to_all | solution.py:21
  117.3 2.4 %collective-permute-start.22 = (f16[32,1024]{1,0:T(8,128)(2,1)S(1)}, f16[32,1024]{1,0:T(8,128)(2,1)S(1)}, u32[]{:S(2)}, u32[]{:S(2)}) collective-permute-start(f16[32,1024]{1,0:T(8,128)(2,1)S(1)} %get-tuple-element.57), channel_id=1, source_target_pairs={{0,192},{32,224},{64,128},{96,160},{128,64},{160,96},{192,0},{224,... | collective-permute-start | bytes 196616 | tf_op jit(solution)/shard_map/ppermute | solution.py:36
  121.8 5.8 %collective-permute-done.18 = f16[32,1024]{1,0:T(8,128)(2,1)S(1)} collective-permute-done((f16[32,1024]{1,0:T(8,128)(2,1)S(1)}, f16[32,1024]{1,0:T(8,128)(2,1)S(1)}, u32[]{:S(2)}, u32[]{:S(2)}) %collective-permute-start.18) | collective-permute-done | bytes 65568 | tf_op jit(solution)/shard_map/ppermute | solution.py:36
  129.0 2.6 %collective-permute-start.19 = (f16[32,1024]{1,0:T(8,128)(2,1)S(1)}, f16[32,1024]{1,0:T(8,128)(2,1)S(1)}, u32[]{:S(2)}, u32[]{:S(2)}) collective-permute-start(f16[32,1024]{1,0:T(8,128)(2,1)S(1)} %get-tuple-element.60), channel_id=1, source_target_pairs={{0,96},{32,0},{64,32},{96,64},{128,224},{160,128},{192,160},{224,1... | collective-permute-start | bytes 196616 | tf_op jit(solution)/shard_map/ppermute | solution.py:36
  134.1 2.2 %collective-permute-start.26 = (f32[8,1024]{1,0:T(8,128)S(1)}, f32[8,1024]{1,0:T(8,128)S(1)}, u32[]{:S(2)}, u32[]{:S(2)}) collective-permute-start(f32[8,1024]{1,0:T(8,128)S(1)} %get-tuple-element.62), channel_id=1, source_target_pairs={{0,16},{8,24},{16,0},{24,8},{1,17},{9,25},{17,1},{25,9},{2,18},{10... | collective-permute-start | bytes 98312 | tf_op jit(solution)/shard_map/ppermute | solution.py:26
  141.8 2.2 %collective-permute-start.29 = (f32[8,1024]{1,0:T(8,128)S(1)}, f32[8,1024]{1,0:T(8,128)S(1)}, u32[]{:S(2)}, u32[]{:S(2)}) collective-permute-start(f32[8,1024]{1,0:T(8,128)S(1)} %get-tuple-element.41), channel_id=1, source_target_pairs={{0,2},{1,3},{2,0},{3,1},{4,6},{5,7},{6,4},{7,5},{8,10},{9,11},{10,... | collective-permute-start | bytes 98312 | tf_op jit(solution)/shard_map/ppermute | solution.py:26
  145.8 2.3 %shard_map.81.looked = f32[64,8192]{1,0:T(8,128)S(1)} custom-call(s32[1]{0:T(128)} %bitcast.place, bf16[16,8,512]{2,1,0:T(8,128)(2,1)S(1)} %all-to-all-done.1.along), custom_call_target="tpu_custom_call" | custom-call | tf_op jit(solution)/shard_map/pallas_call | solution.py:50
  (105 shorter events, 51.3 us)
Async XLA Ops:
  3.8 38.6 %all-to-all-start = ((bf16[16,80,512]{2,1,0:T(8,128)(2,1)}), bf16[16,80,512]{2,1,0:T(8,128)(2,1)S(1)}, u32[]{:S(2)}, u32[]{:S(2)}) async-start(bf16[16,80,512]{2,1,0:T(8,128)(2,1)} %get-tuple-element.26), calls=%async_computation | async-start | bytes 2621440 | tf_op jit(solution)/shard_map/all_to_all | solution.py:21
  18.5 23.0 %collective-permute-start.9 = (bf16[32,1024]{1,0:T(8,128)(2,1)S(1)}, bf16[32,1024]{1,0:T(8,128)(2,1)S(1)}, u32[]{:S(2)}, u32[]{:S(2)}) collective-permute-start(bf16[32,1024]{1,0:T(8,128)(2,1)S(1)} %pad_maximum_fusion.1), channel_id=1, source_target_pairs={{0,224},{32,128},{64,160},{96,192},{128,96},{160,0},{192,32},{224,... | collective-permute-start | bytes 196616 | tf_op jit(solution)/shard_map/ppermute | solution.py:36
  20.0 21.4 %collective-permute-start.8 = (bf16[32,1024]{1,0:T(8,128)(2,1)S(1)}, bf16[32,1024]{1,0:T(8,128)(2,1)S(1)}, u32[]{:S(2)}, u32[]{:S(2)}) collective-permute-start(bf16[32,1024]{1,0:T(8,128)(2,1)S(1)} %pad_maximum_fusion.1), channel_id=1, source_target_pairs={{0,96},{32,0},{64,32},{96,64},{128,224},{160,128},{192,160},{224,1... | collective-permute-start | bytes 196616 | tf_op jit(solution)/shard_map/ppermute | solution.py:36
  22.7 18.7 %collective-permute-start.7 = (bf16[32,1024]{1,0:T(8,128)(2,1)S(1)}, bf16[32,1024]{1,0:T(8,128)(2,1)S(1)}, u32[]{:S(2)}, u32[]{:S(2)}) collective-permute-start(bf16[32,1024]{1,0:T(8,128)(2,1)S(1)} %pad_maximum_fusion.1), channel_id=1, source_target_pairs={{0,192},{32,224},{64,128},{96,160},{128,64},{160,96},{192,0},{224,... | collective-permute-start | bytes 196616 | tf_op jit(solution)/shard_map/ppermute | solution.py:36
  22.9 18.4 %collective-permute-start.6 = (bf16[32,1024]{1,0:T(8,128)(2,1)S(1)}, bf16[32,1024]{1,0:T(8,128)(2,1)S(1)}, u32[]{:S(2)}, u32[]{:S(2)}) collective-permute-start(bf16[32,1024]{1,0:T(8,128)(2,1)S(1)} %pad_maximum_fusion.1), channel_id=1, source_target_pairs={{0,64},{32,96},{64,0},{96,32},{128,192},{160,224},{192,128},{224,1... | collective-permute-start | bytes 196616 | tf_op jit(solution)/shard_map/ppermute | solution.py:36
  41.5 7.7 %collective-permute-start.10 = (bf16[256,1024]{1,0:T(8,128)(2,1)S(1)}, bf16[256,1024]{1,0:T(8,128)(2,1)S(1)}, u32[]{:S(2)}, u32[]{:S(2)}) collective-permute-start(bf16[256,1024]{1,0:T(8,128)(2,1)S(1)} %constant_dynamic-update-slice_fusion.same), channel_id=1, source_target_pairs={{0,4},{4,0},{1,5},{5,1},{2,6},{6,2},{3,7},{7,3},{8,12},{12,8},{9,1... | collective-permute-start | bytes 1572872 | tf_op jit(solution)/shard_map/ppermute | solution.py:26
  42.4 28.5 %all-to-all-start.1 = ((bf16[16,8,512]{2,1,0:T(8,128)(2,1)}), bf16[16,8,512]{2,1,0:T(8,128)(2,1)S(1)}, u32[]{:S(2)}, u32[]{:S(2)}) async-start(bf16[16,8,512]{2,1,0:T(8,128)(2,1)} %maximum_bitcast_fusion), calls=%async_computation.1 | async-start | bytes 262144 | tf_op jit(solution)/shard_map/all_to_all | solution.py:21
  50.6 14.6 %collective-permute-start.11 = (f32[128,512]{1,0:T(8,128)S(1)}, f32[128,512]{1,0:T(8,128)}, u32[]{:S(2)}, u32[]{:S(2)}) collective-permute-start(f32[128,512]{1,0:T(8,128)S(1)} %get-tuple-element.32), channel_id=1, source_target_pairs={{0,24},{8,0},{16,8},{24,16},{1,25},{9,1},{17,9},{25,17},{2,26},{10... | collective-permute-start | bytes 786440 | tf_op jit(solution)/shard_map/ppermute | solution.py:26
  53.6 11.5 %collective-permute-start.12 = (f32[128,512]{1,0:T(8,128)S(1)}, f32[128,512]{1,0:T(8,128)}, u32[]{:S(2)}, u32[]{:S(2)}) collective-permute-start(f32[128,512]{1,0:T(8,128)S(1)} %get-tuple-element.33), channel_id=1, source_target_pairs={{0,16},{8,24},{16,0},{24,8},{1,17},{9,25},{17,1},{25,9},{2,18},{10... | collective-permute-start | bytes 786440 | tf_op jit(solution)/shard_map/ppermute | solution.py:26
  54.1 14.7 %collective-permute-start.13 = (f32[128,512]{1,0:T(8,128)S(1)}, f32[128,512]{1,0:T(8,128)}, u32[]{:S(2)}, u32[]{:S(2)}) collective-permute-start(f32[128,512]{1,0:T(8,128)S(1)} %get-tuple-element.34), channel_id=1, source_target_pairs={{0,8},{8,16},{16,24},{24,0},{1,9},{9,17},{17,25},{25,1},{2,10},{10... | collective-permute-start | bytes 786440 | tf_op jit(solution)/shard_map/ppermute | solution.py:26
  71.5 19.8 %all-to-all-start.2 = ((f32[64,2,128]{2,1,0:T(2,128)}), f32[64,2,128]{2,1,0:T(2,128)S(1)}, u32[]{:S(2)}, u32[]{:S(2)}) async-start(f32[64,2,128]{2,1,0:T(2,128)} %broadcast_in_dim.4), calls=%async_computation.2 | async-start | bytes 131072 | tf_op jit(solution)/shard_map/all_to_all | solution.py:21
  91.6 6.4 %collective-permute-start.16 = (bf16[128,512]{1,0:T(8,128)(2,1)S(1)}, bf16[128,512]{1,0:T(8,128)(2,1)S(1)}, u32[]{:S(2)}, u32[]{:S(2)}) collective-permute-start(bf16[128,512]{1,0:T(8,128)(2,1)S(1)} %fusion.6.g0), channel_id=1, source_target_pairs={{0,24},{8,0},{16,8},{24,16},{1,25},{9,1},{17,9},{25,17},{2,26},{10... | collective-permute-start | bytes 393224 | tf_op jit(solution)/shard_map/ppermute | solution.py:26
  92.4 7.9 %collective-permute-start.15 = (bf16[128,512]{1,0:T(8,128)(2,1)S(1)}, bf16[128,512]{1,0:T(8,128)(2,1)S(1)}, u32[]{:S(2)}, u32[]{:S(2)}) collective-permute-start(bf16[128,512]{1,0:T(8,128)(2,1)S(1)} %fusion.6.g0), channel_id=1, source_target_pairs={{0,16},{8,24},{16,0},{24,8},{1,17},{9,25},{17,1},{25,9},{2,18},{10... | collective-permute-start | bytes 393224 | tf_op jit(solution)/shard_map/ppermute | solution.py:26
  92.9 9.1 %collective-permute-start.14 = (bf16[128,512]{1,0:T(8,128)(2,1)S(1)}, bf16[128,512]{1,0:T(8,128)(2,1)S(1)}, u32[]{:S(2)}, u32[]{:S(2)}) collective-permute-start(bf16[128,512]{1,0:T(8,128)(2,1)S(1)} %fusion.6.g0), channel_id=1, source_target_pairs={{0,8},{8,16},{16,24},{24,0},{1,9},{9,17},{17,25},{25,1},{2,10},{10... | collective-permute-start | bytes 393224 | tf_op jit(solution)/shard_map/ppermute | solution.py:26
  104.6 6.9 %collective-permute-start.17 = (f32[256,1024]{1,0:T(8,128)}, f32[256,1024]{1,0:T(8,128)}, u32[]{:S(2)}, u32[]{:S(2)}) collective-permute-start(f32[256,1024]{1,0:T(8,128)} %get-tuple-element.38), channel_id=1, source_target_pairs={{0,4},{4,0},{1,5},{5,1},{2,6},{6,2},{3,7},{7,3},{8,12},{12,8},{9,1... | collective-permute-start | bytes 3145736 | tf_op jit(solution)/shard_map/ppermute | solution.py:26
  106.7 41.4 %all-to-all-start.3 = ((bf16[16,64,512]{2,1,0:T(8,128)(2,1)}), bf16[16,64,512]{2,1,0:T(8,128)(2,1)S(1)}, u32[]{:S(2)}, u32[]{:S(2)}) async-start(bf16[16,64,512]{2,1,0:T(8,128)(2,1)} %bitcast.39), calls=%async_computation.3 | async-start | bytes 2097152 | tf_op jit(solution)/shard_map/all_to_all | solution.py:21
  113.1 14.5 %collective-permute-start.18 = (f16[32,1024]{1,0:T(8,128)(2,1)S(1)}, f16[32,1024]{1,0:T(8,128)(2,1)S(1)}, u32[]{:S(2)}, u32[]{:S(2)}) collective-permute-start(f16[32,1024]{1,0:T(8,128)(2,1)S(1)} %get-tuple-element.54), channel_id=1, source_target_pairs={{0,128},{32,160},{64,192},{96,224},{128,0},{160,32},{192,64},{224,... | collective-permute-start | bytes 196616 | tf_op jit(solution)/shard_map/ppermute | solution.py:36
  114.7 14.3 %collective-permute-start.24 = (f16[32,1024]{1,0:T(8,128)(2,1)S(1)}, f16[32,1024]{1,0:T(8,128)(2,1)S(1)}, u32[]{:S(2)}, u32[]{:S(2)}) collective-permute-start(f16[32,1024]{1,0:T(8,128)(2,1)S(1)} %get-tuple-element.55), channel_id=1, source_target_pairs={{0,160},{32,192},{64,224},{96,128},{128,32},{160,64},{192,96},{224... | collective-permute-start | bytes 196616 | tf_op jit(solution)/shard_map/ppermute | solution.py:36
  116.1 15.5 %collective-permute-start.23 = (f16[32,1024]{1,0:T(8,128)(2,1)S(1)}, f16[32,1024]{1,0:T(8,128)(2,1)S(1)}, u32[]{:S(2)}, u32[]{:S(2)}) collective-permute-start(f16[32,1024]{1,0:T(8,128)(2,1)S(1)} %get-tuple-element.56), channel_id=1, source_target_pairs={{0,32},{32,64},{64,96},{96,0},{128,160},{160,192},{192,224},{224,1... | collective-permute-start | bytes 196616 | tf_op jit(solution)/shard_map/ppermute | solution.py:36
  117.3 14.6 %collective-permute-start.22 = (f16[32,1024]{1,0:T(8,128)(2,1)S(1)}, f16[32,1024]{1,0:T(8,128)(2,1)S(1)}, u32[]{:S(2)}, u32[]{:S(2)}) collective-permute-start(f16[32,1024]{1,0:T(8,128)(2,1)S(1)} %get-tuple-element.57), channel_id=1, source_target_pairs={{0,192},{32,224},{64,128},{96,160},{128,64},{160,96},{192,0},{224,... | collective-permute-start | bytes 196616 | tf_op jit(solution)/shard_map/ppermute | solution.py:36
  119.7 12.2 %collective-permute-start.21 = (f16[32,1024]{1,0:T(8,128)(2,1)S(1)}, f16[32,1024]{1,0:T(8,128)(2,1)S(1)}, u32[]{:S(2)}, u32[]{:S(2)}) collective-permute-start(f16[32,1024]{1,0:T(8,128)(2,1)S(1)} %get-tuple-element.58), channel_id=1, source_target_pairs={{0,64},{32,96},{64,0},{96,32},{128,192},{160,224},{192,128},{224,1... | collective-permute-start | bytes 196616 | tf_op jit(solution)/shard_map/ppermute | solution.py:36
  140.5 9.1 %collective-permute-start.28 = (f32[8,1024]{1,0:T(8,128)S(1)}, f32[8,1024]{1,0:T(8,128)S(1)}, u32[]{:S(2)}, u32[]{:S(2)}) collective-permute-start(f32[8,1024]{1,0:T(8,128)S(1)} %get-tuple-element.40), channel_id=1, source_target_pairs={{0,1},{1,2},{2,3},{3,0},{4,5},{5,6},{6,7},{7,4},{8,9},{9,10},{10,1... | collective-permute-start | bytes 98312 | tf_op jit(solution)/shard_map/ppermute | solution.py:26
  141.8 8.0 %collective-permute-start.29 = (f32[8,1024]{1,0:T(8,128)S(1)}, f32[8,1024]{1,0:T(8,128)S(1)}, u32[]{:S(2)}, u32[]{:S(2)}) collective-permute-start(f32[8,1024]{1,0:T(8,128)S(1)} %get-tuple-element.41), channel_id=1, source_target_pairs={{0,2},{1,3},{2,0},{3,1},{4,6},{5,7},{6,4},{7,5},{8,10},{9,11},{10,... | collective-permute-start | bytes 98312 | tf_op jit(solution)/shard_map/ppermute | solution.py:26
  144.0 5.8 %collective-permute-start.30 = (f32[8,1024]{1,0:T(8,128)S(1)}, f32[8,1024]{1,0:T(8,128)S(1)}, u32[]{:S(2)}, u32[]{:S(2)}) collective-permute-start(f32[8,1024]{1,0:T(8,128)S(1)} %get-tuple-element.42), channel_id=1, source_target_pairs={{0,3},{1,0},{2,1},{3,2},{4,7},{5,4},{6,5},{7,6},{8,11},{9,8},{10,9... | collective-permute-start | bytes 98312 | tf_op jit(solution)/shard_map/ppermute | solution.py:26
  (11 other events, 55.3 us)

commit v3 on v1

--- a/solution.py
+++ b/solution.py
@@ -114,12 +114,12 @@
         number = jnp.where(line == t, ids[t], number)
     number = jnp.where(lane == rows, number // 256, lax.rem(number, 256))
     number = jnp.where((lane == rows) | (lane == rows + 1), number, 0)
-    number = number.astype(jnp.float32).astype(jnp.bfloat16)
-    for q in range(block // 128):
+    number = number.astype(jnp.float32)
+    for q in range(4):
         piece = weight.astype(jnp.bfloat16)
         weight = weight - piece.astype(jnp.float32)
-        for j in range(cols):
-            stacked[j, rows + own :, q * 128 : (q + 1) * 128] = piece
+        number = jnp.where(lane == rows + 2 + q, piece.astype(jnp.float32), number)
+    number = number.astype(jnp.bfloat16)
     moves[0].wait()
     moves[1].wait()
     for k, out in enumerate(outs):
@@ -243,14 +243,12 @@
 
     stacked, *pieces = call(
         functools.partial(send_kernel, sizes=shape),
-        [held((cols, rows + 2 * own, block), bf16)] + [held((own, 2 * part + 128), bf16)] * ny,
+        [held((cols, rows + own, block), bf16)] + [held((own, 2 * part + 128), bf16)] * ny,
         [pltpu.VMEM((own, width), bf16)] * 2 + [pltpu.SemaphoreType.DMA((2 + 2 * cols,))],
         [SMEM, SMEM, HBM, HBM, HBM, HBM],
     )(place, token_ids, loss_weight, hidden, embed_grad, head, teacher_logits)
     stacked = exchange(stacked, COLS)
     teacher = stacked[:, rows : rows + own].reshape(group, block).astype(f32)
-    weights = stacked[:, rows + own :, :: block // 4].reshape(group, 4).astype(f32)
-    weights = weights[:, 0] + weights[:, 1] + weights[:, 2] + weights[:, 3]
 
     line = [pieces[0]] + [shifted(pieces[k], "y", k) for k in range(1, ny)]
     embed_part = jnp.stack([piece[:, part:] for piece in line])
@@ -287,6 +285,8 @@
     )
     stats = jnp.broadcast_to(stats[None], (cols * nv, *stats.shape))
     stats, along = lax.optimization_barrier((stats, along))
+    weights = along[:, :, rows + 2 : rows + 6].reshape(group, 4).astype(f32)
+    weights = weights[:, 0] + weights[:, 1] + weights[:, 2] + weights[:, 3]
     norms = joined(exchange(stats, COLS + ("vocab",)))
     gap = (
         weights[:, None]

time: 153 us -> 151 us (0.987)
  local copies, waits for them, and re-layouts: 7.18 us -> 1.51 us
  waiting for transfers between devices: 51.8 us -> 55.9 us
    ppermute x17, waiting for transfers between devices: 21.6 us -> 27.8 us  [shifted(): return lax.ppermute(x, axis, [(k, (k + step) % size) for k in range(size)])]
    unnamed x10, local copies, waits for them, and re-layouts: 3.69 us -> 0.34 us
    slice x1, local copies, waits for them, and re-layouts: 1.79 us -> 0.11 us  [per_device(): weights = weights[:, 0] + weights[:, 1] + weights[:, 2] + weights[:, 3]]
    ppermute x14, waiting for transfers between devices: 21.7 us -> 20.2 us  [shifted_both(): return lax.ppermute(x, ('z', 'x'), pairs)]
  transfers between devices with their start and end apart: 35 -> 35, of which waited for: 20 -> 20; matrix products, arithmetic and copies ran while one was open for 9% -> 5% of each run, Pallas kernels for 3% -> 4%
where the time goes in v3:
time: 151 us; the launch traced here: 148 us
  starting transfers between devices  71.5 us (47%)
  waiting for transfers between devices  55.9 us (37%)
  Pallas kernels  11.3 us (7%)
  other arithmetic  5.12 us (3%)
  matrix products  1.91 us (1%)
  local copies, waits for them, and re-layouts  1.51 us (1%)
    all_to_all x4, starting transfers between devices, exchange(): return lax.all_to_all(x, axes, 0, 0, tiled=True)  28.8 us
    ppermute x17, waiting for transfers between devices, shifted(): return lax.ppermute(x, axis, [(k, (k + step) % size) for k in range(size)])  27.8 us
    ppermute x14, starting transfers between devices, shifted_both(): return lax.ppermute(x, ('z', 'x'), pairs)  22.1 us
    ppermute x17, starting transfers between devices, shifted(): return lax.ppermute(x, axis, [(k, (k + step) % size) for k in range(size)])  20.6 us
    ppermute x14, waiting for transfers between devices, shifted_both(): return lax.ppermute(x, ('z', 'x'), pairs)  20.2 us
    pallas_call x6, Pallas kernels, run(): pl.pallas_call(body, out_shape=[spec.memory_space(out.shape, out.dtype) f...  11.3 us
    all_to_all x4, waiting for transfers between devices, exchange(): return lax.all_to_all(x, axes, 0, 0, tiled=True)  7.93 us
  transfers between devices with their start and end apart: 35, of which 20 were waited for; matrix products, arithmetic and copies ran while one was open for 5% of the time, Pallas kernels for 4%

profile of v3, /device:TPU:2, one launch (start us, length us, event | category | flops | bytes accessed | tf_op | source)
XLA Modules:
  0.0 148.2 jit_solution(9709256267362422125)
XLA Ops:
  0.6 3.4 %shard_map.77 = (bf16[16,72,512]{2,1,0:T(8,128)(2,1)}, bf16[8,2176]{1,0:T(8,128)(2,1)S(1)}, bf16[8,2176]{1,0:T(8,128)(2,1)S(1)}, bf16[8,2176]{1,0:T(8,128)(2,1)S(1)}, bf16[8,2176]{1,0:T(8,128)(2,1)S(1)}) custom-call(s32[1]{0:T(128)} %bitcast.place, s32[8]{0:T(128)} %ids.1, f32[8]{0:T(128)} %weights.1, bf16[8,4096]{1,0:T(8,128)(2,1)} %hidden.1, ...), custom_call_target="tpu_custom_call" | custom-call | tf_op jit(solution)/shard_map/pallas_call | solution.py:50
  4.0 6.2 %all-to-all-start = ((bf16[16,72,512]{2,1,0:T(8,128)(2,1)}), bf16[16,72,512]{2,1,0:T(8,128)(2,1)S(1)}, u32[]{:S(2)}, u32[]{:S(2)}) async-start(bf16[16,72,512]{2,1,0:T(8,128)(2,1)} %get-tuple-element.30), calls=%async_computation | async-start | bytes 2359296 | tf_op jit(solution)/shard_map/all_to_all | solution.py:21
  11.8 2.9 %collective-permute-start.1 = (bf16[8,2176]{1,0:T(8,128)(2,1)S(1)}, bf16[8,2176]{1,0:T(8,128)(2,1)S(1)}, u32[]{:S(2)}, u32[]{:S(2)}) collective-permute-start(bf16[8,2176]{1,0:T(8,128)(2,1)S(1)} %get-tuple-element.28), channel_id=1, source_target_pairs={{0,16},{8,24},{16,0},{24,8},{1,17},{9,25},{17,1},{25,9},{2,18},{10... | collective-permute-start | bytes 104456 | tf_op jit(solution)/shard_map/ppermute | solution.py:26
  20.2 2.7 %collective-permute-start.8 = (bf16[32,1024]{1,0:T(8,128)(2,1)S(1)}, bf16[32,1024]{1,0:T(8,128)(2,1)S(1)}, u32[]{:S(2)}, u32[]{:S(2)}) collective-permute-start(bf16[32,1024]{1,0:T(8,128)(2,1)S(1)} %pad_maximum_fusion.1), channel_id=1, source_target_pairs={{0,96},{32,0},{64,32},{96,64},{128,224},{160,128},{192,160},{224,1... | collective-permute-start | bytes 196616 | tf_op jit(solution)/shard_map/ppermute | solution.py:36
  23.1 3.3 %collective-permute-start.6 = (bf16[32,1024]{1,0:T(8,128)(2,1)S(1)}, bf16[32,1024]{1,0:T(8,128)(2,1)S(1)}, u32[]{:S(2)}, u32[]{:S(2)}) collective-permute-start(bf16[32,1024]{1,0:T(8,128)(2,1)S(1)} %pad_maximum_fusion.1), channel_id=1, source_target_pairs={{0,64},{32,96},{64,0},{96,32},{128,192},{160,224},{192,128},{224,1... | collective-permute-start | bytes 196616 | tf_op jit(solution)/shard_map/ppermute | solution.py:36
  27.9 2.8 %collective-permute-done.3 = bf16[32,1024]{1,0:T(8,128)(2,1)S(1)} collective-permute-done((bf16[32,1024]{1,0:T(8,128)(2,1)S(1)}, bf16[32,1024]{1,0:T(8,128)(2,1)S(1)}, u32[]{:S(2)}, u32[]{:S(2)}) %collective-permute-start.3) | collective-permute-done | bytes 65568 | tf_op jit(solution)/shard_map/ppermute | solution.py:36
  31.3 3.6 %collective-permute-done.4 = bf16[32,1024]{1,0:T(8,128)(2,1)S(1)} collective-permute-done((bf16[32,1024]{1,0:T(8,128)(2,1)S(1)}, bf16[32,1024]{1,0:T(8,128)(2,1)S(1)}, u32[]{:S(2)}, u32[]{:S(2)}) %collective-permute-start.4) | collective-permute-done | bytes 65568 | tf_op jit(solution)/shard_map/ppermute | solution.py:36
  35.9 4.3 %collective-permute-done.5 = bf16[32,1024]{1,0:T(8,128)(2,1)S(1)} collective-permute-done((bf16[32,1024]{1,0:T(8,128)(2,1)S(1)}, bf16[32,1024]{1,0:T(8,128)(2,1)S(1)}, u32[]{:S(2)}, u32[]{:S(2)}) %collective-permute-start.5) | collective-permute-done | bytes 65568 | tf_op jit(solution)/shard_map/ppermute | solution.py:36
  41.5 6.5 %all-to-all-start.1 = ((bf16[16,8,512]{2,1,0:T(8,128)(2,1)}), bf16[16,8,512]{2,1,0:T(8,128)(2,1)S(1)}, u32[]{:S(2)}, u32[]{:S(2)}) async-start(bf16[16,8,512]{2,1,0:T(8,128)(2,1)} %maximum_bitcast_fusion), calls=%async_computation.1 | async-start | bytes 262144 | tf_op jit(solution)/shard_map/all_to_all | solution.py:21
  49.6 2.6 %collective-permute-start.11 = (f32[128,512]{1,0:T(8,128)S(1)}, f32[128,512]{1,0:T(8,128)}, u32[]{:S(2)}, u32[]{:S(2)}) collective-permute-start(f32[128,512]{1,0:T(8,128)S(1)} %get-tuple-element.32), channel_id=1, source_target_pairs={{0,24},{8,0},{16,8},{24,16},{1,25},{9,1},{17,9},{25,17},{2,26},{10... | collective-permute-start | bytes 786440 | tf_op jit(solution)/shard_map/ppermute | solution.py:26
  53.7 10.0 %collective-permute-done.11 = f32[128,512]{1,0:T(8,128)} collective-permute-done((f32[128,512]{1,0:T(8,128)S(1)}, f32[128,512]{1,0:T(8,128)}, u32[]{:S(2)}, u32[]{:S(2)}) %collective-permute-start.11) | collective-permute-done | bytes 262176 | tf_op jit(solution)/shard_map/ppermute | solution.py:26
  63.7 3.5 %collective-permute-done.13 = f32[128,512]{1,0:T(8,128)} collective-permute-done((f32[128,512]{1,0:T(8,128)S(1)}, f32[128,512]{1,0:T(8,128)}, u32[]{:S(2)}, u32[]{:S(2)}) %collective-permute-start.13) | collective-permute-done | bytes 262176 | tf_op jit(solution)/shard_map/ppermute | solution.py:26
  69.3 11.2 %all-to-all-start.2 = ((f32[64,2,128]{2,1,0:T(2,128)}), f32[64,2,128]{2,1,0:T(2,128)S(1)}, u32[]{:S(2)}, u32[]{:S(2)}) async-start(f32[64,2,128]{2,1,0:T(2,128)} %broadcast_in_dim.4), calls=%async_computation.2 | async-start | bytes 131072 | tf_op jit(solution)/shard_map/all_to_all | solution.py:21
  81.0 7.9 %all-to-all-done.2 = f32[64,2,128]{2,1,0:T(2,128)S(1)} async-done(((f32[64,2,128]{2,1,0:T(2,128)}), f32[64,2,128]{2,1,0:T(2,128)S(1)}, u32[]{:S(2)}, u32[]{:S(2)}) %all-to-all-start.2) | async-done | bytes 65568 | tf_op jit(solution)/shard_map/all_to_all | solution.py:21
  91.3 4.3 %collective-permute-done.16.g3 = bf16[128,512]{1,0:T(8,128)(2,1)S(1)} collective-permute-done((bf16[128,512]{1,0:T(8,128)(2,1)S(1)}, bf16[128,512]{1,0:T(8,128)(2,1)S(1)}, u32[]{:S(2)}, u32[]{:S(2)}) %collective-permute-start.16) | collective-permute-done | bytes 131104 | tf_op jit(solution)/shard_map/ppermute | solution.py:26
  95.6 2.4 %collective-permute-done.15.g2 = bf16[128,512]{1,0:T(8,128)(2,1)S(1)} collective-permute-done((bf16[128,512]{1,0:T(8,128)(2,1)S(1)}, bf16[128,512]{1,0:T(8,128)(2,1)S(1)}, u32[]{:S(2)}, u32[]{:S(2)}) %collective-permute-start.15) | collective-permute-done | bytes 131104 | tf_op jit(solution)/shard_map/ppermute | solution.py:26
  99.7 2.7 %shard_map.79 = (f32[256,1024]{1,0:T(8,128)S(1)}, f32[256,1024]{1,0:T(8,128)}, bf16[512,512]{1,0:T(8,128)(2,1)S(1)}) custom-call(s32[1]{0:T(128)} %bitcast.place, bf16[128,512]{1,0:T(8,128)(2,1)S(1)} %fusion.6.g0, bf16[128,512]{1,0:T(8,128)(2,1)S(1)} %collective-permute-done.14.g1, bf16[128,512]{1,0:T(8,128)(2,1)S(1)} %collective-permute-done.15.g2, ...), custom_call_target="tpu_custom_call" | custom-call | tf_op jit(solution)/shard_map/pallas_call | solution.py:50
  104.4 4.9 %all-to-all-start.3 = ((bf16[16,64,512]{2,1,0:T(8,128)(2,1)}), bf16[16,64,512]{2,1,0:T(8,128)(2,1)S(1)}, u32[]{:S(2)}, u32[]{:S(2)}) async-start(bf16[16,64,512]{2,1,0:T(8,128)(2,1)} %bitcast.39), calls=%async_computation.3 | async-start | bytes 2097152 | tf_op jit(solution)/shard_map/all_to_all | solution.py:21
  115.0 2.4 %collective-permute-start.22 = (f16[32,1024]{1,0:T(8,128)(2,1)S(1)}, f16[32,1024]{1,0:T(8,128)(2,1)S(1)}, u32[]{:S(2)}, u32[]{:S(2)}) collective-permute-start(f16[32,1024]{1,0:T(8,128)(2,1)S(1)} %get-tuple-element.57), channel_id=1, source_target_pairs={{0,192},{32,224},{64,128},{96,160},{128,64},{160,96},{192,0},{224,... | collective-permute-start | bytes 196616 | tf_op jit(solution)/shard_map/ppermute | solution.py:36
  117.4 2.1 %collective-permute-start.21 = (f16[32,1024]{1,0:T(8,128)(2,1)S(1)}, f16[32,1024]{1,0:T(8,128)(2,1)S(1)}, u32[]{:S(2)}, u32[]{:S(2)}) collective-permute-start(f16[32,1024]{1,0:T(8,128)(2,1)S(1)} %get-tuple-element.58), channel_id=1, source_target_pairs={{0,64},{32,96},{64,0},{96,32},{128,192},{160,224},{192,128},{224,1... | collective-permute-start | bytes 196616 | tf_op jit(solution)/shard_map/ppermute | solution.py:36
  119.5 5.8 %collective-permute-done.18 = f16[32,1024]{1,0:T(8,128)(2,1)S(1)} collective-permute-done((f16[32,1024]{1,0:T(8,128)(2,1)S(1)}, f16[32,1024]{1,0:T(8,128)(2,1)S(1)}, u32[]{:S(2)}, u32[]{:S(2)}) %collective-permute-start.18) | collective-permute-done | bytes 65568 | tf_op jit(solution)/shard_map/ppermute | solution.py:36
  126.8 2.6 %collective-permute-start.19 = (f16[32,1024]{1,0:T(8,128)(2,1)S(1)}, f16[32,1024]{1,0:T(8,128)(2,1)S(1)}, u32[]{:S(2)}, u32[]{:S(2)}) collective-permute-start(f16[32,1024]{1,0:T(8,128)(2,1)S(1)} %get-tuple-element.60), channel_id=1, source_target_pairs={{0,96},{32,0},{64,32},{96,64},{128,224},{160,128},{192,160},{224,1... | collective-permute-start | bytes 196616 | tf_op jit(solution)/shard_map/ppermute | solution.py:36
  139.6 2.2 %collective-permute-start.29 = (f32[8,1024]{1,0:T(8,128)S(1)}, f32[8,1024]{1,0:T(8,128)S(1)}, u32[]{:S(2)}, u32[]{:S(2)}) collective-permute-start(f32[8,1024]{1,0:T(8,128)S(1)} %get-tuple-element.42), channel_id=1, source_target_pairs={{0,2},{1,3},{2,0},{3,1},{4,6},{5,7},{6,4},{7,5},{8,10},{9,11},{10,... | collective-permute-start | bytes 98312 | tf_op jit(solution)/shard_map/ppermute | solution.py:26
  143.5 2.3 %shard_map.81.looked = f32[64,8192]{1,0:T(8,128)S(1)} custom-call(s32[1]{0:T(128)} %bitcast.place, bf16[16,8,512]{2,1,0:T(8,128)(2,1)S(1)} %all-to-all-done.1.along), custom_call_target="tpu_custom_call" | custom-call | tf_op jit(solution)/shard_map/pallas_call | solution.py:50
  (104 shorter events, 44.7 us)
Async XLA Ops:
  4.0 37.4 %all-to-all-start = ((bf16[16,72,512]{2,1,0:T(8,128)(2,1)}), bf16[16,72,512]{2,1,0:T(8,128)(2,1)S(1)}, u32[]{:S(2)}, u32[]{:S(2)}) async-start(bf16[16,72,512]{2,1,0:T(8,128)(2,1)} %get-tuple-element.30), calls=%async_computation | async-start | bytes 2359296 | tf_op jit(solution)/shard_map/all_to_all | solution.py:21
  18.7 21.6 %collective-permute-start.9 = (bf16[32,1024]{1,0:T(8,128)(2,1)S(1)}, bf16[32,1024]{1,0:T(8,128)(2,1)S(1)}, u32[]{:S(2)}, u32[]{:S(2)}) collective-permute-start(bf16[32,1024]{1,0:T(8,128)(2,1)S(1)} %pad_maximum_fusion.1), channel_id=1, source_target_pairs={{0,224},{32,128},{64,160},{96,192},{128,96},{160,0},{192,32},{224,... | collective-permute-start | bytes 196616 | tf_op jit(solution)/shard_map/ppermute | solution.py:36
  20.2 20.0 %collective-permute-start.8 = (bf16[32,1024]{1,0:T(8,128)(2,1)S(1)}, bf16[32,1024]{1,0:T(8,128)(2,1)S(1)}, u32[]{:S(2)}, u32[]{:S(2)}) collective-permute-start(bf16[32,1024]{1,0:T(8,128)(2,1)S(1)} %pad_maximum_fusion.1), channel_id=1, source_target_pairs={{0,96},{32,0},{64,32},{96,64},{128,224},{160,128},{192,160},{224,1... | collective-permute-start | bytes 196616 | tf_op jit(solution)/shard_map/ppermute | solution.py:36
  22.9 17.3 %collective-permute-start.7 = (bf16[32,1024]{1,0:T(8,128)(2,1)S(1)}, bf16[32,1024]{1,0:T(8,128)(2,1)S(1)}, u32[]{:S(2)}, u32[]{:S(2)}) collective-permute-start(bf16[32,1024]{1,0:T(8,128)(2,1)S(1)} %pad_maximum_fusion.1), channel_id=1, source_target_pairs={{0,192},{32,224},{64,128},{96,160},{128,64},{160,96},{192,0},{224,... | collective-permute-start | bytes 196616 | tf_op jit(solution)/shard_map/ppermute | solution.py:36
  23.1 17.0 %collective-permute-start.6 = (bf16[32,1024]{1,0:T(8,128)(2,1)S(1)}, bf16[32,1024]{1,0:T(8,128)(2,1)S(1)}, u32[]{:S(2)}, u32[]{:S(2)}) collective-permute-start(bf16[32,1024]{1,0:T(8,128)(2,1)S(1)} %pad_maximum_fusion.1), channel_id=1, source_target_pairs={{0,64},{32,96},{64,0},{96,32},{128,192},{160,224},{192,128},{224,1... | collective-permute-start | bytes 196616 | tf_op jit(solution)/shard_map/ppermute | solution.py:36
  40.3 7.9 %collective-permute-start.10 = (bf16[256,1024]{1,0:T(8,128)(2,1)S(1)}, bf16[256,1024]{1,0:T(8,128)(2,1)S(1)}, u32[]{:S(2)}, u32[]{:S(2)}) collective-permute-start(bf16[256,1024]{1,0:T(8,128)(2,1)S(1)} %constant_dynamic-update-slice_fusion.same), channel_id=1, source_target_pairs={{0,4},{4,0},{1,5},{5,1},{2,6},{6,2},{3,7},{7,3},{8,12},{12,8},{9,1... | collective-permute-start | bytes 1572872 | tf_op jit(solution)/shard_map/ppermute | solution.py:26
  41.5 27.2 %all-to-all-start.1 = ((bf16[16,8,512]{2,1,0:T(8,128)(2,1)}), bf16[16,8,512]{2,1,0:T(8,128)(2,1)S(1)}, u32[]{:S(2)}, u32[]{:S(2)}) async-start(bf16[16,8,512]{2,1,0:T(8,128)(2,1)} %maximum_bitcast_fusion), calls=%async_computation.1 | async-start | bytes 262144 | tf_op jit(solution)/shard_map/all_to_all | solution.py:21
  49.6 14.1 %collective-permute-start.11 = (f32[128,512]{1,0:T(8,128)S(1)}, f32[128,512]{1,0:T(8,128)}, u32[]{:S(2)}, u32[]{:S(2)}) collective-permute-start(f32[128,512]{1,0:T(8,128)S(1)} %get-tuple-element.32), channel_id=1, source_target_pairs={{0,24},{8,0},{16,8},{24,16},{1,25},{9,1},{17,9},{25,17},{2,26},{10... | collective-permute-start | bytes 786440 | tf_op jit(solution)/shard_map/ppermute | solution.py:26
  52.2 11.5 %collective-permute-start.12 = (f32[128,512]{1,0:T(8,128)S(1)}, f32[128,512]{1,0:T(8,128)}, u32[]{:S(2)}, u32[]{:S(2)}) collective-permute-start(f32[128,512]{1,0:T(8,128)S(1)} %get-tuple-element.33), channel_id=1, source_target_pairs={{0,16},{8,24},{16,0},{24,8},{1,17},{9,25},{17,1},{25,9},{2,18},{10... | collective-permute-start | bytes 786440 | tf_op jit(solution)/shard_map/ppermute | solution.py:26
  52.4 14.7 %collective-permute-start.13 = (f32[128,512]{1,0:T(8,128)S(1)}, f32[128,512]{1,0:T(8,128)}, u32[]{:S(2)}, u32[]{:S(2)}) collective-permute-start(f32[128,512]{1,0:T(8,128)S(1)} %get-tuple-element.34), channel_id=1, source_target_pairs={{0,8},{8,16},{16,24},{24,0},{1,9},{9,17},{17,25},{25,1},{2,10},{10... | collective-permute-start | bytes 786440 | tf_op jit(solution)/shard_map/ppermute | solution.py:26
  69.3 19.6 %all-to-all-start.2 = ((f32[64,2,128]{2,1,0:T(2,128)}), f32[64,2,128]{2,1,0:T(2,128)S(1)}, u32[]{:S(2)}, u32[]{:S(2)}) async-start(f32[64,2,128]{2,1,0:T(2,128)} %broadcast_in_dim.4), calls=%async_computation.2 | async-start | bytes 131072 | tf_op jit(solution)/shard_map/all_to_all | solution.py:21
  89.2 6.4 %collective-permute-start.16 = (bf16[128,512]{1,0:T(8,128)(2,1)S(1)}, bf16[128,512]{1,0:T(8,128)(2,1)S(1)}, u32[]{:S(2)}, u32[]{:S(2)}) collective-permute-start(bf16[128,512]{1,0:T(8,128)(2,1)S(1)} %fusion.6.g0), channel_id=1, source_target_pairs={{0,24},{8,0},{16,8},{24,16},{1,25},{9,1},{17,9},{25,17},{2,26},{10... | collective-permute-start | bytes 393224 | tf_op jit(solution)/shard_map/ppermute | solution.py:26
  90.1 7.9 %collective-permute-start.15 = (bf16[128,512]{1,0:T(8,128)(2,1)S(1)}, bf16[128,512]{1,0:T(8,128)(2,1)S(1)}, u32[]{:S(2)}, u32[]{:S(2)}) collective-permute-start(bf16[128,512]{1,0:T(8,128)(2,1)S(1)} %fusion.6.g0), channel_id=1, source_target_pairs={{0,16},{8,24},{16,0},{24,8},{1,17},{9,25},{17,1},{25,9},{2,18},{10... | collective-permute-start | bytes 393224 | tf_op jit(solution)/shard_map/ppermute | solution.py:26
  90.4 9.3 %collective-permute-start.14 = (bf16[128,512]{1,0:T(8,128)(2,1)S(1)}, bf16[128,512]{1,0:T(8,128)(2,1)S(1)}, u32[]{:S(2)}, u32[]{:S(2)}) collective-permute-start(bf16[128,512]{1,0:T(8,128)(2,1)S(1)} %fusion.6.g0), channel_id=1, source_target_pairs={{0,8},{8,16},{16,24},{24,0},{1,9},{9,17},{17,25},{25,1},{2,10},{10... | collective-permute-start | bytes 393224 | tf_op jit(solution)/shard_map/ppermute | solution.py:26
  102.4 6.9 %collective-permute-start.17 = (f32[256,1024]{1,0:T(8,128)}, f32[256,1024]{1,0:T(8,128)}, u32[]{:S(2)}, u32[]{:S(2)}) collective-permute-start(f32[256,1024]{1,0:T(8,128)} %get-tuple-element.39), channel_id=1, source_target_pairs={{0,4},{4,0},{1,5},{5,1},{2,6},{6,2},{3,7},{7,3},{8,12},{12,8},{9,1... | collective-permute-start | bytes 3145736 | tf_op jit(solution)/shard_map/ppermute | solution.py:26
  104.4 41.4 %all-to-all-start.3 = ((bf16[16,64,512]{2,1,0:T(8,128)(2,1)}), bf16[16,64,512]{2,1,0:T(8,128)(2,1)S(1)}, u32[]{:S(2)}, u32[]{:S(2)}) async-start(bf16[16,64,512]{2,1,0:T(8,128)(2,1)} %bitcast.39), calls=%async_computation.3 | async-start | bytes 2097152 | tf_op jit(solution)/shard_map/all_to_all | solution.py:21
  110.8 14.5 %collective-permute-start.18 = (f16[32,1024]{1,0:T(8,128)(2,1)S(1)}, f16[32,1024]{1,0:T(8,128)(2,1)S(1)}, u32[]{:S(2)}, u32[]{:S(2)}) collective-permute-start(f16[32,1024]{1,0:T(8,128)(2,1)S(1)} %get-tuple-element.54), channel_id=1, source_target_pairs={{0,128},{32,160},{64,192},{96,224},{128,0},{160,32},{192,64},{224,... | collective-permute-start | bytes 196616 | tf_op jit(solution)/shard_map/ppermute | solution.py:36
  112.4 14.3 %collective-permute-start.24 = (f16[32,1024]{1,0:T(8,128)(2,1)S(1)}, f16[32,1024]{1,0:T(8,128)(2,1)S(1)}, u32[]{:S(2)}, u32[]{:S(2)}) collective-permute-start(f16[32,1024]{1,0:T(8,128)(2,1)S(1)} %get-tuple-element.55), channel_id=1, source_target_pairs={{0,160},{32,192},{64,224},{96,128},{128,32},{160,64},{192,96},{224... | collective-permute-start | bytes 196616 | tf_op jit(solution)/shard_map/ppermute | solution.py:36
  113.8 15.5 %collective-permute-start.23 = (f16[32,1024]{1,0:T(8,128)(2,1)S(1)}, f16[32,1024]{1,0:T(8,128)(2,1)S(1)}, u32[]{:S(2)}, u32[]{:S(2)}) collective-permute-start(f16[32,1024]{1,0:T(8,128)(2,1)S(1)} %get-tuple-element.56), channel_id=1, source_target_pairs={{0,32},{32,64},{64,96},{96,0},{128,160},{160,192},{192,224},{224,1... | collective-permute-start | bytes 196616 | tf_op jit(solution)/shard_map/ppermute | solution.py:36
  115.0 14.6 %collective-permute-start.22 = (f16[32,1024]{1,0:T(8,128)(2,1)S(1)}, f16[32,1024]{1,0:T(8,128)(2,1)S(1)}, u32[]{:S(2)}, u32[]{:S(2)}) collective-permute-start(f16[32,1024]{1,0:T(8,128)(2,1)S(1)} %get-tuple-element.57), channel_id=1, source_target_pairs={{0,192},{32,224},{64,128},{96,160},{128,64},{160,96},{192,0},{224,... | collective-permute-start | bytes 196616 | tf_op jit(solution)/shard_map/ppermute | solution.py:36
  117.4 12.2 %collective-permute-start.21 = (f16[32,1024]{1,0:T(8,128)(2,1)S(1)}, f16[32,1024]{1,0:T(8,128)(2,1)S(1)}, u32[]{:S(2)}, u32[]{:S(2)}) collective-permute-start(f16[32,1024]{1,0:T(8,128)(2,1)S(1)} %get-tuple-element.58), channel_id=1, source_target_pairs={{0,64},{32,96},{64,0},{96,32},{128,192},{160,224},{192,128},{224,1... | collective-permute-start | bytes 196616 | tf_op jit(solution)/shard_map/ppermute | solution.py:36
  138.2 9.1 %collective-permute-start.28 = (f32[8,1024]{1,0:T(8,128)S(1)}, f32[8,1024]{1,0:T(8,128)S(1)}, u32[]{:S(2)}, u32[]{:S(2)}) collective-permute-start(f32[8,1024]{1,0:T(8,128)S(1)} %get-tuple-element.41), channel_id=1, source_target_pairs={{0,1},{1,2},{2,3},{3,0},{4,5},{5,6},{6,7},{7,4},{8,9},{9,10},{10,1... | collective-permute-start | bytes 98312 | tf_op jit(solution)/shard_map/ppermute | solution.py:26
  139.6 8.0 %collective-permute-start.29 = (f32[8,1024]{1,0:T(8,128)S(1)}, f32[8,1024]{1,0:T(8,128)S(1)}, u32[]{:S(2)}, u32[]{:S(2)}) collective-permute-start(f32[8,1024]{1,0:T(8,128)S(1)} %get-tuple-element.42), channel_id=1, source_target_pairs={{0,2},{1,3},{2,0},{3,1},{4,6},{5,7},{6,4},{7,5},{8,10},{9,11},{10,... | collective-permute-start | bytes 98312 | tf_op jit(solution)/shard_map/ppermute | solution.py:26
  141.8 5.8 %collective-permute-start.30 = (f32[8,1024]{1,0:T(8,128)S(1)}, f32[8,1024]{1,0:T(8,128)S(1)}, u32[]{:S(2)}, u32[]{:S(2)}) collective-permute-start(f32[8,1024]{1,0:T(8,128)S(1)} %get-tuple-element.43), channel_id=1, source_target_pairs={{0,3},{1,0},{2,1},{3,2},{4,7},{5,4},{6,5},{7,6},{8,11},{9,8},{10,9... | collective-permute-start | bytes 98312 | tf_op jit(solution)/shard_map/ppermute | solution.py:26
  (11 other events, 54.0 us)
